TPU v7x, 32 devices: a whole 2x2x4 slice. The times are simulated.
32 devices in a mesh: pipe: 4 (over z), dp: 4 (over y, x), tensor: 2 (over core).
Axes of the slice: x: 2, y: 2, z: 4, core: 2. Of those that a mesh axis runs over, the one named last changes fastest.
Arguments:
- saved_inputs: bfloat16 [3, 2, 4, 512, 4096], P(None, None, 'pipe', 'dp', 'tensor'), may hold values from -6 to 6
- proj_in: bfloat16 [2, 4, 512, 4096], P(None, 'pipe', None, 'tensor'), may hold values from -0.09375 to 0.09375
- proj_out: bfloat16 [2, 4, 512, 4096], P(None, 'pipe', None, 'tensor'), may hold values from -0.25 to 0.25
- norm_gain: float32 [2, 4, 4096], P(None, 'pipe', 'tensor'), may hold values from 0.1 to 1.9
- arriving: bfloat16 [2, 4, 512, 4096], P(None, 'pipe', 'dp', 'tensor'), may hold values from -6 to 6
- logp_grad: bfloat16 [2, 512, 4096], P(None, 'dp', 'tensor'), may hold values from -6 to 6
- rewards: float32 [2, 4, 4], P(None, 'dp'), may hold values from -4 to 4
- seq_lengths: int32 [2, 4, 4], P(None, 'dp'), may hold values from 1 to 64, 128 in all within a row
- group_ids: int32 [2, 4, 4], P(None, 'dp'), may hold values from 0 to 3
Outputs:
- grad_in: float32 [2, 4, 512, 4096], P(None, 'pipe', 'dp', 'tensor')
- grad_out: float32 [2, 4, 512, 4096], P(None, 'pipe', 'dp', 'tensor')
- leaving: bfloat16 [2, 4, 512, 4096], P(None, 'pipe', 'dp', 'tensor')
Inputs may be any that keep to these rules, and one draw needn't show every extreme that they name: `seq_lengths`: the 4 lengths of one microbatch on one replica sum to 128. `group_ids`: groups take sequences from several replicas and microbatches.
All inputs are finite; a program needn't handle non-finite values.
Results may differ from a plain program's by a relative error of at most 0.023.
Values may be sent and summed in bfloat16 or wider, within the bound.
No kernel may reach another device: no remote copies, remote signals or barrier semaphores. Data moves between devices by JAX's collectives and lax.ppermute only.
A program may use at most 128 MiB of HBM per device.

v0:
```python
import functools

import jax
import jax.numpy as jnp
from jax import lax
from jax.experimental import pallas as pl
from jax.experimental.pallas import tpu as pltpu
from jax.sharding import PartitionSpec as P


EPS = 1e-05
LANES = 128
START_LIMIT = 46<<20


VMEM = pl.BlockSpec(memory_space=pltpu.VMEM)
SMEM = pl.BlockSpec(memory_space=pltpu.SMEM)
HBM = pl.BlockSpec(memory_space=pltpu.HBM)


def call(kernel, outs, operands, flops, scratch=(), specs=None, limit=8 << 20):
    return pl.pallas_call(
        kernel,
        out_shape=outs,
        in_specs=specs or [VMEM] * len(operands),
        out_specs=jax.tree.map(lambda _: VMEM, outs),
        scratch_shapes=list(scratch),
        compiler_params=pltpu.CompilerParams(vmem_limit_bytes=limit),
        cost_estimate=pl.CostEstimate(flops=flops, bytes_accessed=0, transcendentals=0),
    )(*operands)


def shape(dims, dtype):
    return jax.ShapeDtypeStruct(tuple(dims), dtype)


def dot(left, right, dims):
    return lax.dot_general(left, right, (dims, ((), ())), preferred_element_type=jnp.float32)


def moved_by(x, axis, by):
    count = lax.axis_size(axis)
    return lax.ppermute(x, axis, [(i, (i + by) % count) for i in range(count)])


def with_peers(part, axis):
    count = lax.axis_size(axis)
    parts = [part]
    for by in range(1, count):
        to = (lambda i: i ^ by) if count & (count - 1) == 0 else (lambda i: (i + by) % count)
        parts.append(lax.ppermute(part, axis, [(i, to(i)) for i in range(count)]))
    return parts


class Pairing:
    def __init__(self, lowest):
        self.count = lax.axis_size("dp")
        self.groups = self.count // 2
        self.lowest = lowest

    def place(self):
        me = lax.axis_index("dp")
        if self.lowest:
            return lax.rem(me, 2), me // 2
        return me // self.groups, lax.rem(me, self.groups)

    def index(self, g, b):
        return g * 2 + b if self.lowest else b * self.groups + g

    def to_partner(self, x):
        pairs = [
            (self.index(g, b), self.index(g, 1 - b)) for g in range(self.groups) for b in range(2)
        ]
        return lax.ppermute(x, "dp", pairs)

    def to_group(self, x, by):
        pairs = [
            (self.index(g, b), self.index((g + by) % self.groups, b))
            for g in range(self.groups)
            for b in range(2)
        ]
        return lax.ppermute(x, "dp", pairs)

    def starts(self, b, piece):
        return [pl.multiple_of(self.index(g, b) * piece, piece) for g in range(self.groups)]


def tiles_of(width):
    tile = 512 if width % 512 == 0 else LANES
    return [slice(at, at + tile) for at in range(0, width, tile)]


def pre_rows(saved, v, weight_of, gain_ref):
    ref, at = saved
    _, rows, width = ref.shape
    total = None
    squares = jnp.zeros((rows, 1), jnp.float32)
    for cut in tiles_of(width):
        x = ref[at, :, cut].astype(jnp.float32)
        squares = squares + jnp.sum(x * x, axis=-1, keepdims=True)
        gained = (x * gain_ref[v, :, cut]).astype(jnp.bfloat16)
        term = dot(gained, weight_of(cut), ((1,), (1,)))
        total = term if total is None else total + term
    lane = lax.broadcasted_iota(jnp.int32, (rows, LANES), 1)
    high = squares.astype(jnp.bfloat16).astype(jnp.float32)
    return total.astype(jnp.bfloat16), jnp.where(lane == 0, high, squares - high).astype(jnp.bfloat16)


def start_kernel(v, loads, count, saved_ref, proj_in_ref, proj_out_ref, gain_ref, cot_ref, *refs):
    given, refs = refs[: len(refs) - count - 1], refs[len(refs) - count - 1 :]
    out_ref, win_ref, wout_ref, tokens, sems = refs[0], refs[1], refs[2], refs[3:-1], refs[-1]
    pairs = [(proj_out_ref.at[v, 0], wout_ref)]
    pairs += [(saved_ref.at[0, w, 0], target.at[0]) for w, target in zip(loads, tokens)]
    pairs += [(proj_in_ref.at[v, 0], win_ref)]
    copies = [
        pltpu.make_async_copy(source, target, sems.at[i]) for i, (source, target) in enumerate(pairs)
    ]
    for copy in copies:
        copy.start()
    rows = cot_ref.shape[0]
    rank = win_ref.shape[0]
    copies[0].wait()
    out_ref[rows:, :rank] = dot(cot_ref[...], wout_ref[...], ((1,), (1,))).astype(jnp.bfloat16)
    out_ref[rows:, rank:] = jnp.zeros((rows, LANES), jnp.bfloat16)
    for copy in copies[1:]:
        copy.wait()
    mine = given[0] if given else tokens[0]
    value, squares = pre_rows((mine, 0), v, lambda cut: win_ref[:, cut], gain_ref)
    out_ref[:rows, :rank] = value
    out_ref[:rows, rank:] = squares


def pre_kernel(v, at, saved_ref, win_ref, gain_ref, out_ref):
    rank = win_ref.shape[0]
    value, squares = pre_rows((saved_ref, at), v, lambda cut: win_ref[:, cut], gain_ref)
    out_ref[:, :rank] = value
    out_ref[:, rank:] = squares


def upper_kernel(sections, t, got_ref, entering_ref, wout_ref, cot_ref, part_ref):
    is_top = lax.axis_index("pipe") == sections - 1

    @pl.when(is_top)
    def _():
        cot_ref[...] = entering_ref[t]

    @pl.when(jnp.logical_not(is_top))
    def _():
        cot_ref[...] = got_ref[...]

    part_ref[...] = dot(cot_ref[...], wout_ref[...], ((1,), (1,))).astype(jnp.bfloat16)


def lower_kernel(got_ref, wout_ref, part_ref):
    part_ref[...] = dot(got_ref[...], wout_ref[...], ((1,), (1,))).astype(jnp.bfloat16)


def half_weight(ref, pairing, cut):
    piece = ref.shape[0] // pairing.count
    b, _ = pairing.place()
    return jnp.concatenate([ref[pl.ds(at, piece), cut] for at in pairing.starts(b, piece)], axis=0)


def partner_kernel(v, pairing, first_ref, later_ref, cot_ref, win_ref, wout_ref, gain_ref, out_ref):
    later_steps, rows, width = later_ref.shape
    steps = later_steps + 1
    half = win_ref.shape[0] // 2
    for t in range(steps):
        place = slice(t * rows, (t + 1) * rows)
        saved = (later_ref, t - 1) if t else (first_ref, 0)
        value, squares = pre_rows(saved, v, lambda cut: half_weight(win_ref, pairing, cut), gain_ref)
        out_ref[place, :half] = value
        out_ref[place, half:] = squares
    place = slice(steps * rows, (steps + 1) * rows)
    weight = half_weight(wout_ref, pairing, slice(0, width))
    out_ref[place, :half] = dot(cot_ref[...], weight, ((1,), (1,))).astype(jnp.bfloat16)
    out_ref[place, half:] = jnp.zeros((rows, LANES), jnp.bfloat16)


def partner_back_kernel(pairing, cot_ref, wout_ref, out_ref):
    weight = half_weight(wout_ref, pairing, slice(0, cot_ref.shape[1]))
    out_ref[...] = dot(cot_ref[...], weight, ((1,), (1,))).astype(jnp.bfloat16)


def summed(parts, where, columns):
    result = parts[0][where, columns].astype(jnp.float32)
    for ref in parts[1:]:
        result = result + ref[where, columns].astype(jnp.float32)
    return result


def activation(parts, where, rank, full_width):
    pre_sum = summed(parts, where, slice(0, rank))
    squares = summed(parts, where, slice(rank, rank + LANES))
    squares = squares[:, 0:1] + squares[:, 1:2]
    inv_rms = 1.0 / jnp.sqrt(squares / full_width + EPS)
    pre = inv_rms * pre_sum
    return pre_sum, inv_rms, pre, jax.nn.sigmoid(pre)


def slope(pre, sigma):
    return sigma * (1.0 + pre * (1.0 - sigma))


def step_kernel(v, saved_at, at, back_at, peers, full_width, pairing, mode, *refs):
    firsts, backs, refs = refs[:peers], refs[peers : 2 * peers], refs[2 * peers :]
    cot_ref, saved_ref, win_ref, gain_ref, refs = *refs[:4], refs[4:]
    if mode != "plain":
        other_ref, refs = refs[0], refs[1:]
    out_ref, mine_ref, turned = refs
    rows, width = saved_ref.shape[1:]
    rank = win_ref.shape[0]
    where = slice(at * rows, (at + 1) * rows)
    pre_sum, inv_rms, pre, sigma = activation(firsts, where, rank, full_width)
    back_sum = summed(backs, slice(back_at * rows, (back_at + 1) * rows), slice(0, rank))
    hidden = (pre * sigma).astype(jnp.bfloat16)
    grad_pre = back_sum * slope(pre, sigma)
    scaled = (inv_rms * grad_pre).astype(jnp.bfloat16)
    radial = jnp.sum(grad_pre * pre_sum, axis=-1, keepdims=True)
    pull = inv_rms * inv_rms * inv_rms * radial / full_width

    for cut in tiles_of(width):
        result = (
            cot_ref[:, cut].astype(jnp.float32)
            + gain_ref[v, :, cut] * dot(scaled, win_ref[:, cut], ((1,), (0,)))
            - saved_ref[saved_at, :, cut].astype(jnp.float32) * pull
        ).astype(jnp.bfloat16)
        if mode == "both":
            out_ref[0, :, cut] = result
            out_ref[1, :, cut] = other_ref[:, cut]
        else:
            out_ref[:, cut] = result
    if mode == "bottom":

        @pl.when(lax.axis_index("pipe") == 0)
        def _():
            out_ref[...] = other_ref[...]

    b, _ = pairing.place()
    piece = rank // pairing.count
    for k, value in enumerate((scaled, hidden)):
        turned[k] = value.T
        for g, start in enumerate(pairing.starts(b, piece)):
            mine_ref[k, g * piece : (g + 1) * piece] = turned[k, pl.ds(start, piece)]


def grad_kernel(k, v, steps, peers, full_width, pairing, operands, *refs):
    mine, refs = refs[:steps], refs[steps:]
    firsts, refs = refs[:peers], refs[peers:]
    backs = [[firsts, steps]]
    if k == 0:
        for _ in range(1, steps):
            backs.append([refs[:peers], 0])
            refs = refs[peers:]
    rights, refs = refs[:operands], refs[operands:]
    own_ref, sends, turned = refs[0], refs[1:-1], refs[-1]
    half, rows = mine[0].shape[1:]
    for t in range(steps):
        where = slice(t * rows, (t + 1) * rows)
        _, inv_rms, pre, sigma = activation(firsts, where, half, full_width)
        if k:
            value = pre * sigma
        else:
            parts, at = backs[t]
            back_sum = summed(parts, slice(at * rows, (at + 1) * rows), slice(0, half))
            value = inv_rms * (back_sum * slope(pre, sigma))
        turned[t] = value.astype(jnp.bfloat16).T
    _, g = pairing.place()
    piece = half // pairing.groups
    width = own_ref.shape[1]
    lefts = []
    for t in range(steps):
        chunks = []
        for by in range(pairing.groups):
            at = pl.ds(pl.multiple_of(lax.rem(g + by, pairing.groups) * piece, piece), piece)
            chunks.append(jnp.concatenate([mine[t][k, at], turned[t, at]], axis=1))
        lefts.append(jnp.concatenate(chunks, axis=0))
    for cut in tiles_of(width):
        total = None
        for t in range(steps):
            if k:
                pair = [rights[t][:, cut], rights[steps + t][:, cut]]
            else:
                gain = rights[4][v, :, cut]
                refs_at = ((rights[1], t - 1), (rights[3], t - 1)) if t else ((rights[0], 0), (rights[2], 0))
                pair = [
                    (ref[at, :, cut].astype(jnp.float32) * gain).astype(jnp.bfloat16) for ref, at in refs_at
                ]
            term = dot(lefts[t], jnp.concatenate(pair, axis=0), ((1,), (0,)))
            total = term if total is None else total + term
        own_ref[:, cut] = total[:piece]
        for by in range(1, pairing.groups):
            sends[by - 1][:, cut] = total[by * piece : (by + 1) * piece].astype(jnp.bfloat16)


def final_kernel(scale, count, *refs):
    out_ref = refs[-1]
    for v in range(2):
        parts = refs[v * count : (v + 1) * count]
        total = parts[0][...]
        for ref in parts[1:]:
            total = total + ref[...].astype(jnp.float32)
        out_ref[v] = total * scale


def stats_kernel(rewards_ref, ids_ref, out_ref):
    new_count, _, seq_count = rewards_ref.shape
    lane = lax.broadcasted_iota(jnp.int32, (1, LANES), 1)
    sums = jnp.zeros((1, LANES), jnp.float32)
    counts = jnp.zeros((1, LANES), jnp.float32)
    for n in range(new_count):
        for k in range(seq_count):
            hit = lane == ids_ref[n, 0, k]
            sums = sums + jnp.where(hit, rewards_ref[n, 0, k], 0.0)
            counts = counts + jnp.where(hit, 1.0, 0.0)
    out_ref[...] = jnp.zeros_like(out_ref)
    out_ref[0:1] = sums
    out_ref[1:2] = counts


def entering_kernel(parts, rewards_ref, ids_ref, lengths_ref, logp_ref, *refs):
    out_ref = refs[-1]
    new_count, _, seq_count = rewards_ref.shape
    rows = logp_ref.shape[1]
    total = refs[0][...]
    for ref in refs[1:parts]:
        total = total + ref[...]
    means = total[0:1] / jnp.maximum(total[1:2], 1.0)
    lane = lax.broadcasted_iota(jnp.int32, (1, LANES), 1)
    position = lax.broadcasted_iota(jnp.int32, (rows, 1), 0)
    for n in range(new_count):
        weight = jnp.zeros((rows, 1), jnp.float32)
        start = jnp.int32(0)
        for k in range(seq_count):
            end = start + lengths_ref[n, 0, k]
            mean = jnp.sum(jnp.where(lane == ids_ref[n, 0, k], means, 0.0), axis=-1, keepdims=True)
            inside = jnp.logical_and(position >= start, position < end)
            weight = weight + jnp.where(inside, rewards_ref[n, 0, k] - mean, 0.0)
            start = end
        out_ref[n] = (-weight * logp_ref[n].astype(jnp.float32)).astype(jnp.bfloat16)


def shards(
    saved_inputs, proj_in, proj_out, norm_gain, arriving, logp_grad, rewards, seq_lengths, group_ids
):
    sections = lax.axis_size("pipe")
    replicas = lax.axis_size("dp")
    peers = lax.axis_size("tensor")
    first_cots = [arriving[v, 0] for v in range(2)]
    later_saved = [saved_inputs[1:, v, 0] for v in range(2)]
    steps, rows, width = saved_inputs.shape[0], *later_saved[0].shape[1:]
    full_width = width * peers
    rank = proj_in.shape[2]
    half = rank // 2
    piece = rank // replicas
    new_count = logp_grad.shape[0]
    pairings = [Pairing(True), Pairing(False)]
    bf16, f32 = jnp.bfloat16, jnp.float32
    product = 2 * rows * rank * width

    def partner(v, x):
        return pairings[v].to_partner(x)

    stats = call(stats_kernel, shape((8, LANES), f32), (rewards, group_ids), 1000, specs=[SMEM, SMEM])
    entering = call(
        functools.partial(entering_kernel, replicas),
        shape((new_count, rows, width), bf16),
        (rewards, group_ids, seq_lengths, logp_grad, *with_peers(stats, "dp")),
        product // 4,
        specs=[SMEM] * 3 + [VMEM] * (1 + replicas),
    )

    cots = [first_cots]
    theirs_c = [[partner(v, first_cots[v]) for v in range(2)]]

    firsts, laters, w_in, w_out = [None] * 2, [[None], [None]], [None] * 2, [None] * 2
    for v in (1, 0):
        loads = (1, 0) if v else ()
        part, w_in[v], w_out[v], *tokens = call(
            functools.partial(start_kernel, v, loads, 3 + len(loads)),
            [shape((2 * rows, rank + LANES), bf16)]
            + [shape((rank, width), bf16)] * 2
            + [shape((1, rows, width), bf16)] * len(loads),
            (saved_inputs, proj_in, proj_out, norm_gain, first_cots[v]) + (() if v else (first_saved[0],)),
            2 * product,
            scratch=[pltpu.SemaphoreType.DMA((2 + len(loads),))],
            specs=[HBM] * 3 + [VMEM] * (2 if v else 3),
            limit=START_LIMIT,
        )
        if v:
            first_saved = tokens[::-1]
        firsts[v] = with_peers(part, "tensor")
    theirs_first = [partner(v, first_saved[v]) for v in range(2)]
    theirs_later = [partner(v, later_saved[v]) for v in range(2)]
    for t in range(1, steps):
        for v in (1, 0):
            part = call(
                functools.partial(pre_kernel, v, t - 1),
                shape((rows, rank + LANES), bf16),
                (later_saved[v], w_in[v], norm_gain),
                product,
            )
            laters[v].append(with_peers(part, "tensor"))

    def finish(v, t, backs, mode, other):
        operands = (*(laters[v][t] if t else firsts[v]), *backs, cots[t][v])
        operands += (later_saved[v] if t else first_saved[v], w_in[v], norm_gain)
        if mode != "plain":
            operands = operands + (other,)
        at, back_at = max(t - 1, 0), 0 if t else 1
        return call(
            functools.partial(step_kernel, v, at, 0, back_at, peers, full_width, pairings[v], mode),
            [shape((2, rows, width) if mode == "both" else (rows, width), bf16), shape((2, half, rows), bf16)],
            operands,
            product,
            scratch=[pltpu.VMEM((2, rank, rows), bf16)],
        )

    mine, backs = [], firsts
    line = [(s, s - 1) for s in range(1, sections)]
    for t in range(steps):
        now, side = [None] * 2, [None] * 2
        last = t + 1 == steps
        for v in (1, 0):
            mode = "plain" if v else ("both" if last else "bottom")
            now[v], side[v] = finish(v, t, backs[v], mode, now[1])
        mine.append(side)
        if last:
            leaving = now[0]
            break
        upper = lax.ppermute(now[1], "pipe", line)
        lower = moved_by(now[0], "pipe", -1)
        cot_upper, part = call(
            functools.partial(upper_kernel, sections, t),
            [shape((rows, width), bf16), shape((rows, rank), bf16)],
            (upper, entering, w_out[1]),
            product,
        )
        backs = [None, with_peers(part, "tensor")]
        part = call(lower_kernel, shape((rows, rank), bf16), (lower, w_out[0]), product)
        backs[0] = with_peers(part, "tensor")
        cots.append([lower, cot_upper])
        theirs_c.append([partner(v, cots[t + 1][v]) for v in range(2)])

    peer_firsts, peer_backs = [None, None], [[], []]
    for v in (1, 0):
        part = call(
            functools.partial(partner_kernel, v, pairings[v]),
            shape(((steps + 1) * rows, half + LANES), bf16),
            (theirs_first[v], theirs_later[v], theirs_c[0][v], w_in[v], w_out[v], norm_gain),
            (steps + 1) * product // 2,
        )
        peer_firsts[v] = with_peers(part, "tensor")
        for t in range(1, steps):
            part = call(
                functools.partial(partner_back_kernel, pairings[v]),
                shape((rows, half), bf16),
                (theirs_c[t][v], w_out[v]),
                product // 2,
            )
            peer_backs[v] += with_peers(part, "tensor")

    scale = 1.0 / (replicas * rows)
    grads = []
    for k in (0, 1):
        parts = []
        for v in range(2):
            if k:
                rights = tuple(cots[t][v] for t in range(steps)) + tuple(theirs_c[t][v] for t in range(steps))
            else:
                rights = tuple(peer_backs[v])
                rights += (first_saved[v], later_saved[v], theirs_first[v], theirs_later[v], norm_gain)
            own, *sends = call(
                functools.partial(
                    grad_kernel, k, v, steps, peers, full_width, pairings[v], 2 * steps if k else 5
                ),
                [shape((piece, width), f32)] + [shape((piece, width), bf16)] * (pairings[v].groups - 1),
                tuple(mine[t][v] for t in range(steps)) + tuple(peer_firsts[v]) + rights,
                steps * product,
                scratch=[pltpu.VMEM((steps, half, rows), bf16)],
            )
            parts += [own] + [pairings[v].to_group(send, by + 1) for by, send in enumerate(sends)]
        grads.append(
            call(
                functools.partial(final_kernel, scale, len(parts) // 2),
                shape((2, piece, width), f32),
                tuple(parts),
                product // 8,
            )
        )
    return (grads[0][:, None], grads[1][:, None], leaving[:, None])


def solution(mesh):
    return jax.shard_map(
        shards,
        mesh=mesh,
        in_specs=(
            P(None, None, "pipe", "dp", "tensor"),
            P(None, "pipe", None, "tensor"),
            P(None, "pipe", None, "tensor"),
            P(None, "pipe", "tensor"),
            P(None, "pipe", "dp", "tensor"),
            P(None, "dp", "tensor"),
            P(None, "dp", None),
            P(None, "dp", None),
            P(None, "dp", None),
        ),
        out_specs=(
            P(None, "pipe", "dp", "tensor"),
            P(None, "pipe", "dp", "tensor"),
            P(None, "pipe", "dp", "tensor"),
        ),
        check_vma=False,
    )
```

profile of v0, /device:TPU:0, one launch (start us, length us, event | category | flops | bytes accessed | tf_op | source)
XLA Modules:
  0.0 135.8 jit_solution(301606683879206865)
XLA Ops:
  1.9 3.4 %shard_map.112 = (bf16[256,640]{1,0:T(8,128)(2,1)S(1)}, bf16[512,2048]{1,0:T(8,128)(2,1)S(1)}, bf16[512,2048]{1,0:T(8,128)(2,1)S(1)}, bf16[1,128,2048]{2,1,0:T(8,128)(2,1)S(1)}, bf16[1,128,2048]{2,1,0:T(8,128)(2,1)S(1)}) custom-call(bf16[3,2,1,128,2048]{4,3,2,1,0:T(8,128)(2,1)} %saved_ref.3, bf16[2,1,512,2048]{3,2,1,0:T(8,128)(2,1)} %proj_in_ref.3, ...), custom_call_target="tpu_custom_call" | custom-call | flops 536870912 | tf_op jit(solution)/shard_map/pallas_call | solution.py:22
  5.9 3.4 %shard_map.113 = (bf16[256,640]{1,0:T(8,128)(2,1)S(1)}, bf16[512,2048]{1,0:T(8,128)(2,1)S(1)}, bf16[512,2048]{1,0:T(8,128)(2,1)S(1)}) custom-call(bf16[3,2,1,128,2048]{4,3,2,1,0:T(8,128)(2,1)} %saved_ref.3, bf16[2,1,512,2048]{3,2,1,0:T(8,128)(2,1)} %proj_in_ref.3, bf16[2,1,512,2048]{3,2,1,0:T(8,128)(2,1)} %proj_out_ref.3, f32[2,1,2048]{2,1,0:T(1,128)S(1)} %copy-done, ...), custom_call_target="tpu_custom_call" | custom-call | flops 536870912 | tf_op jit(solution)/shard_map/pallas_call | solution.py:22
  14.1 5.7 %collective-permute-start.3 = (bf16[128,2048]{1,0:T(8,128)(2,1)S(1)}, bf16[128,2048]{1,0:T(8,128)(2,1)S(1)}, u32[]{:S(2)}, u32[]{:S(2)}) collective-permute-start(bf16[128,2048]{1,0:T(8,128)(2,1)S(1)} %get-tuple-element.43), channel_id=1, source_target_pairs={{0,24},{8,0},{16,8},{24,16},{1,25},{9,1},{17,9},{25,17},{2,26},{10... | collective-permute-start | bytes 1572872 | tf_op jit(solution)/shard_map/ppermute | solution.py:43
  20.4 2.5 %collective-permute-start.9 = (f32[8,128]{1,0:T(8,128)S(1)}, f32[8,128]{1,0:T(8,128)S(1)}, u32[]{:S(2)}, u32[]{:S(2)}) collective-permute-start(f32[8,128]{1,0:T(8,128)S(1)} %shard_map.119.refs_0_), channel_id=1, source_target_pairs={{0,6},{2,4},{4,2},{6,0},{1,7},{3,5},{5,3},{7,1},{8,14},{10,12},{12... | collective-permute-start | bytes 12296 | tf_op jit(solution)/shard_map/ppermute | solution.py:51
  23.4 1.6 %collective-permute-done.9.refs_3_ = f32[8,128]{1,0:T(8,128)S(1)} collective-permute-done((f32[8,128]{1,0:T(8,128)S(1)}, f32[8,128]{1,0:T(8,128)S(1)}, u32[]{:S(2)}, u32[]{:S(2)}) %collective-permute-start.9) | collective-permute-done | bytes 4128 | tf_op jit(solution)/shard_map/ppermute | solution.py:51
  25.0 1.5 %collective-permute-start.7 = (f32[8,128]{1,0:T(8,128)S(1)}, f32[8,128]{1,0:T(8,128)S(1)}, u32[]{:S(2)}, u32[]{:S(2)}) collective-permute-start(f32[8,128]{1,0:T(8,128)S(1)} %shard_map.119.refs_0_), channel_id=1, source_target_pairs={{0,2},{2,0},{4,6},{6,4},{1,3},{3,1},{5,7},{7,5},{8,10},{10,8},{12,... | collective-permute-start | bytes 12296 | tf_op jit(solution)/shard_map/ppermute | solution.py:51
  32.6 1.5 %collective-permute-start.27 = (bf16[2,128,2048]{2,1,0:T(8,128)(2,1)S(1)}, bf16[2,128,2048]{2,1,0:T(8,128)(2,1)S(1)}, u32[]{:S(2)}, u32[]{:S(2)}) collective-permute-start(bf16[2,128,2048]{2,1,0:T(8,128)(2,1)S(1)} %get-tuple-element.70.saved_ref.refs_5_.refs_10_), channel_id=1, source_target_pairs={{0,4},{4,0},{2,6},{6,2},{1,5},{5,1},{3,7},{7,3},{8,12},{12,8},{10,... | collective-permute-start | bytes 3145736 | tf_op jit(solution)/shard_map/ppermute | solution.py:74
  36.8 3.3 %collective-permute-done.3.got_ref.refs_4_.refs_6_ = bf16[128,2048]{1,0:T(8,128)(2,1)S(1)} collective-permute-done((bf16[128,2048]{1,0:T(8,128)(2,1)S(1)}, bf16[128,2048]{1,0:T(8,128)(2,1)S(1)}, u32[]{:S(2)}, u32[]{:S(2)}) %collective-permute-start.3) | collective-permute-done | bytes 524320 | tf_op jit(solution)/shard_map/ppermute | solution.py:43
  41.5 1.8 %collective-permute-done.19.cot_ref.refs_8_ = bf16[128,2048]{1,0:T(8,128)(2,1)S(1)} collective-permute-done((bf16[128,2048]{1,0:T(8,128)(2,1)S(1)}, bf16[128,2048]{1,0:T(8,128)(2,1)S(1)}, u32[]{:S(2)}, u32[]{:S(2)}) %collective-permute-start.19) | collective-permute-done | bytes 524320 | tf_op jit(solution)/shard_map/ppermute | solution.py:74
  48.4 24.5 %collective-permute-done.26.first_ref.refs_11_ = bf16[1,128,2048]{2,1,0:T(8,128)(2,1)S(1)} collective-permute-done((bf16[1,128,2048]{2,1,0:T(8,128)(2,1)S(1)}, bf16[1,128,2048]{2,1,0:T(8,128)(2,1)S(1)}, u32[]{:S(2)}, u32[]{:S(2)}) %collective-permute-start.26) | collective-permute-done | bytes 524320 | tf_op jit(solution)/shard_map/ppermute | solution.py:74
  73.3 5.9 %collective-permute-done.17.first_ref.refs_11_ = bf16[1,128,2048]{2,1,0:T(8,128)(2,1)S(1)} collective-permute-done((bf16[1,128,2048]{2,1,0:T(8,128)(2,1)S(1)}, bf16[1,128,2048]{2,1,0:T(8,128)(2,1)S(1)}, u32[]{:S(2)}, u32[]{:S(2)}) %collective-permute-start.17) | collective-permute-done | bytes 524320 | tf_op jit(solution)/shard_map/ppermute | solution.py:74
  80.4 1.5 %collective-permute-start.21 = (bf16[128,2048]{1,0:T(8,128)(2,1)S(1)}, bf16[128,2048]{1,0:T(8,128)(2,1)S(1)}, u32[]{:S(2)}, u32[]{:S(2)}) collective-permute-start(bf16[128,2048]{1,0:T(8,128)(2,1)S(1)} %collective-permute-done.3.got_ref.refs_4_.refs_6_), channel_id=1, source_target_pairs={{0,2},{2,0},{4,6},{6,4},{1,3},{3,1},{5,7},{7,5},{8,10},{10,8},{12,... | collective-permute-start | bytes 1572872 | tf_op jit(solution)/shard_map/ppermute | solution.py:74
  85.1 1.6 %shard_map.134.refs_3_ = bf16[512,384]{1,0:T(8,128)(2,1)S(1)} custom-call(bf16[1,128,2048]{2,1,0:T(8,128)(2,1)S(1)} %collective-permute-done.26.first_ref.refs_11_, bf16[2,128,2048]{2,1,0:T(8,128)(2,1)S(1)} %collective-permute-done.27.later_ref.refs_12_, bf16[128,2048]{1,0:T(8,128)(2,1)S(1)} %collective-permute-done.28.cot_ref.refs_8_, ...), custom_call_target="tpu_custom_call" | custom-call | flops 536870912 | tf_op jit(solution)/shard_map/pallas_call | solution.py:22
  86.8 1.6 %shard_map.130.refs_3_ = bf16[512,384]{1,0:T(8,128)(2,1)S(1)} custom-call(bf16[1,128,2048]{2,1,0:T(8,128)(2,1)S(1)} %collective-permute-done.17.first_ref.refs_11_, bf16[2,128,2048]{2,1,0:T(8,128)(2,1)S(1)} %collective-permute-done.18.later_ref.refs_12_, bf16[128,2048]{1,0:T(8,128)(2,1)S(1)} %collective-permute-done.19.cot_ref.refs_8_, ...), custom_call_target="tpu_custom_call" | custom-call | flops 536870912 | tf_op jit(solution)/shard_map/pallas_call | solution.py:22
  88.4 5.5 %collective-permute-done.30.cot_ref.refs_9_ = bf16[128,2048]{1,0:T(8,128)(2,1)S(1)} collective-permute-done((bf16[128,2048]{1,0:T(8,128)(2,1)S(1)}, bf16[128,2048]{1,0:T(8,128)(2,1)S(1)}, u32[]{:S(2)}, u32[]{:S(2)}) %collective-permute-start.30) | collective-permute-done | bytes 524320 | tf_op jit(solution)/shard_map/ppermute | solution.py:74
  98.9 1.8 %shard_map.129 = (bf16[2,128,2048]{2,1,0:T(8,128)(2,1)}, bf16[2,256,128]{2,1,0:T(8,128)(2,1)S(1)}) custom-call(bf16[128,640]{1,0:T(8,128)(2,1)S(1)} %shard_map.124.refs_0_, bf16[128,640]{1,0:T(8,128)(2,1)S(1)} %collective-permute-done.11.refs_1_, bf16[128,512]{1,0:T(8,128)(2,1)S(1)} %shard_map.125.refs_2_, ...), custom_call_target="tpu_custom_call" | custom-call | flops 268435456 | tf_op jit(solution)/shard_map/pallas_call | solution.py:22
  100.7 2.1 %collective-permute-done.32.cot_ref.refs_10_ = bf16[128,2048]{1,0:T(8,128)(2,1)S(1)} collective-permute-done((bf16[128,2048]{1,0:T(8,128)(2,1)S(1)}, bf16[128,2048]{1,0:T(8,128)(2,1)S(1)}, u32[]{:S(2)}, u32[]{:S(2)}) %collective-permute-start.32) | collective-permute-done | bytes 524320 | tf_op jit(solution)/shard_map/ppermute | solution.py:74
  108.6 1.6 %collective-permute-start.35 = (bf16[128,2048]{1,0:T(8,128)(2,1)S(1)}, bf16[128,2048]{1,0:T(8,128)(2,1)S(1)}, u32[]{:S(2)}, u32[]{:S(2)}) collective-permute-start(bf16[128,2048]{1,0:T(8,128)(2,1)S(1)} %get-tuple-element.63), channel_id=1, source_target_pairs={{0,4},{2,6},{4,0},{6,2},{1,5},{3,7},{5,1},{7,3},{8,12},{10,14},{12... | collective-permute-start | bytes 1572872 | tf_op jit(solution)/shard_map/ppermute | solution.py:82
  114.3 5.8 %collective-permute-done.36.refs_3_ = bf16[128,2048]{1,0:T(8,128)(2,1)S(1)} collective-permute-done((bf16[128,2048]{1,0:T(8,128)(2,1)S(1)}, bf16[128,2048]{1,0:T(8,128)(2,1)S(1)}, u32[]{:S(2)}, u32[]{:S(2)}) %collective-permute-start.36) | collective-permute-done | bytes 524320 | tf_op jit(solution)/shard_map/ppermute | solution.py:82
  120.2 3.3 %collective-permute-done.35.refs_1_ = bf16[128,2048]{1,0:T(8,128)(2,1)S(1)} collective-permute-done((bf16[128,2048]{1,0:T(8,128)(2,1)S(1)}, bf16[128,2048]{1,0:T(8,128)(2,1)S(1)}, u32[]{:S(2)}, u32[]{:S(2)}) %collective-permute-start.35) | collective-permute-done | bytes 524320 | tf_op jit(solution)/shard_map/ppermute | solution.py:82
  123.5 1.5 %shard_map.141 = f32[2,128,2048]{2,1,0:T(8,128)} custom-call(f32[128,2048]{1,0:T(8,128)S(1)} %get-tuple-element.62.refs_0_, bf16[128,2048]{1,0:T(8,128)(2,1)S(1)} %collective-permute-done.35.refs_1_, f32[128,2048]{1,0:T(8,128)S(1)} %get-tuple-element.64.refs_2_, bf16[128,2048]{1,0:T(8,128)(2,1)S(1)} %collective-permute-done.36.refs_3_), custom_call_target="tpu_custom_call" | custom-call | flops 33554432 | tf_op jit(solution)/shard_map/pallas_call | solution.py:22
  125.0 5.4 %collective-permute-done.34.refs_3_ = bf16[128,2048]{1,0:T(8,128)(2,1)S(1)} collective-permute-done((bf16[128,2048]{1,0:T(8,128)(2,1)S(1)}, bf16[128,2048]{1,0:T(8,128)(2,1)S(1)}, u32[]{:S(2)}, u32[]{:S(2)}) %collective-permute-start.34) | collective-permute-done | bytes 524320 | tf_op jit(solution)/shard_map/ppermute | solution.py:82
  130.4 3.8 %collective-permute-done.25.refs_1_ = bf16[128,2048]{1,0:T(8,128)(2,1)S(1)} collective-permute-done((bf16[128,2048]{1,0:T(8,128)(2,1)S(1)}, bf16[128,2048]{1,0:T(8,128)(2,1)S(1)}, u32[]{:S(2)}, u32[]{:S(2)}) %collective-permute-start.25) | collective-permute-done | bytes 524320 | tf_op jit(solution)/shard_map/ppermute | solution.py:82
  134.2 1.5 %shard_map.138 = f32[2,128,2048]{2,1,0:T(8,128)} custom-call(f32[128,2048]{1,0:T(8,128)S(1)} %get-tuple-element.55.refs_0_, bf16[128,2048]{1,0:T(8,128)(2,1)S(1)} %collective-permute-done.25.refs_1_, f32[128,2048]{1,0:T(8,128)S(1)} %get-tuple-element.60.refs_2_, bf16[128,2048]{1,0:T(8,128)(2,1)S(1)} %collective-permute-done.34.refs_3_), custom_call_target="tpu_custom_call" | custom-call | flops 33554432 | tf_op jit(solution)/shard_map/pallas_call | solution.py:22
  (94 shorter events, 42.5 us)
Async XLA Ops:
  10.4 18.5 %collective-permute-start.5 = (bf16[128,640]{1,0:T(8,128)(2,1)S(1)}, bf16[128,640]{1,0:T(8,128)(2,1)S(1)}, u32[]{:S(2)}, u32[]{:S(2)}) collective-permute-start(bf16[128,640]{1,0:T(8,128)(2,1)S(1)} %shard_map.118.refs_0_), channel_id=1, source_target_pairs={{0,1},{1,0},{2,3},{3,2},{4,5},{5,4},{6,7},{7,6},{8,9},{9,8},{10,11... | collective-permute-start | bytes 491528 | tf_op jit(solution)/shard_map/ppermute | solution.py:51
  11.8 20.9 %collective-permute-start.6 = (bf16[128,2048]{1,0:T(8,128)(2,1)S(1)}, bf16[128,2048]{1,0:T(8,128)(2,1)S(1)}, u32[]{:S(2)}, u32[]{:S(2)}) collective-permute-start(bf16[128,2048]{1,0:T(8,128)(2,1)S(1)} %get-tuple-element.41.refs_8_), channel_id=1, source_target_pairs={{8,0},{16,8},{24,16},{9,1},{17,9},{25,17},{10,2},{18,10},{26,18},{... | collective-permute-start | bytes 1572872 | tf_op jit(solution)/shard_map/ppermute | solution.py:431
  14.1 26.0 %collective-permute-start.3 = (bf16[128,2048]{1,0:T(8,128)(2,1)S(1)}, bf16[128,2048]{1,0:T(8,128)(2,1)S(1)}, u32[]{:S(2)}, u32[]{:S(2)}) collective-permute-start(bf16[128,2048]{1,0:T(8,128)(2,1)S(1)} %get-tuple-element.43), channel_id=1, source_target_pairs={{0,24},{8,0},{16,8},{24,16},{1,25},{9,1},{17,9},{25,17},{2,26},{10... | collective-permute-start | bytes 1572872 | tf_op jit(solution)/shard_map/ppermute | solution.py:43
  26.5 14.8 %collective-permute-start.28 = (bf16[128,2048]{1,0:T(8,128)(2,1)S(1)}, bf16[128,2048]{1,0:T(8,128)(2,1)S(1)}, u32[]{:S(2)}, u32[]{:S(2)}) collective-permute-start(bf16[128,2048]{1,0:T(8,128)(2,1)S(1)} %get-tuple-element.72.cot_ref.refs_4_.refs_5_), channel_id=1, source_target_pairs={{0,4},{4,0},{2,6},{6,2},{1,5},{5,1},{3,7},{7,3},{8,12},{12,8},{10,... | collective-permute-start | bytes 1572872 | tf_op jit(solution)/shard_map/ppermute | solution.py:74
  28.9 14.3 %collective-permute-start.19 = (bf16[128,2048]{1,0:T(8,128)(2,1)S(1)}, bf16[128,2048]{1,0:T(8,128)(2,1)S(1)}, u32[]{:S(2)}, u32[]{:S(2)}) collective-permute-start(bf16[128,2048]{1,0:T(8,128)(2,1)S(1)} %get-tuple-element.73.cot_ref.refs_4_.refs_5_), channel_id=1, source_target_pairs={{0,2},{2,0},{4,6},{6,4},{1,3},{3,1},{5,7},{7,5},{8,10},{10,8},{12,... | collective-permute-start | bytes 1572872 | tf_op jit(solution)/shard_map/ppermute | solution.py:74
  32.6 50.3 %collective-permute-start.27 = (bf16[2,128,2048]{2,1,0:T(8,128)(2,1)S(1)}, bf16[2,128,2048]{2,1,0:T(8,128)(2,1)S(1)}, u32[]{:S(2)}, u32[]{:S(2)}) collective-permute-start(bf16[2,128,2048]{2,1,0:T(8,128)(2,1)S(1)} %get-tuple-element.70.saved_ref.refs_5_.refs_10_), channel_id=1, source_target_pairs={{0,4},{4,0},{2,6},{6,2},{1,5},{5,1},{3,7},{7,3},{8,12},{12,8},{10,... | collective-permute-start | bytes 3145736 | tf_op jit(solution)/shard_map/ppermute | solution.py:74
  36.2 36.6 %collective-permute-start.26 = (bf16[1,128,2048]{2,1,0:T(8,128)(2,1)S(1)}, bf16[1,128,2048]{2,1,0:T(8,128)(2,1)S(1)}, u32[]{:S(2)}, u32[]{:S(2)}) collective-permute-start(bf16[1,128,2048]{2,1,0:T(8,128)(2,1)S(1)} %get-tuple-element.39.refs_5_.refs_9_), channel_id=1, source_target_pairs={{0,4},{4,0},{2,6},{6,2},{1,5},{5,1},{3,7},{7,3},{8,12},{12,8},{10,... | collective-permute-start | bytes 1572872 | tf_op jit(solution)/shard_map/ppermute | solution.py:74
  43.2 43.5 %collective-permute-start.18 = (bf16[2,128,2048]{2,1,0:T(8,128)(2,1)S(1)}, bf16[2,128,2048]{2,1,0:T(8,128)(2,1)S(1)}, u32[]{:S(2)}, u32[]{:S(2)}) collective-permute-start(bf16[2,128,2048]{2,1,0:T(8,128)(2,1)S(1)} %get-tuple-element.71.saved_ref.refs_5_.refs_10_), channel_id=1, source_target_pairs={{0,2},{2,0},{4,6},{6,4},{1,3},{3,1},{5,7},{7,5},{8,10},{10,8},{12,... | collective-permute-start | bytes 3145736 | tf_op jit(solution)/shard_map/ppermute | solution.py:74
  44.4 34.7 %collective-permute-start.17 = (bf16[1,128,2048]{2,1,0:T(8,128)(2,1)S(1)}, bf16[1,128,2048]{2,1,0:T(8,128)(2,1)S(1)}, u32[]{:S(2)}, u32[]{:S(2)}) collective-permute-start(bf16[1,128,2048]{2,1,0:T(8,128)(2,1)S(1)} %get-tuple-element.35.refs_0_.refs_5_.refs_9_), channel_id=1, source_target_pairs={{0,2},{2,0},{4,6},{6,4},{1,3},{3,1},{5,7},{7,5},{8,10},{10,8},{12,... | collective-permute-start | bytes 1572872 | tf_op jit(solution)/shard_map/ppermute | solution.py:74
  46.1 34.3 %collective-permute-start.15 = (bf16[128,2048]{1,0:T(8,128)(2,1)S(1)}, bf16[128,2048]{1,0:T(8,128)(2,1)S(1)}, u32[]{:S(2)}, u32[]{:S(2)}) collective-permute-start(bf16[128,2048]{1,0:T(8,128)(2,1)S(1)} %get-tuple-element.48.refs_8_), channel_id=1, source_target_pairs={{8,0},{16,8},{24,16},{9,1},{17,9},{25,17},{10,2},{18,10},{26,18},{... | collective-permute-start | bytes 1572872 | tf_op jit(solution)/shard_map/ppermute | solution.py:431
  72.8 11.8 %collective-permute-start.12 = (bf16[128,2048]{1,0:T(8,128)(2,1)S(1)}, bf16[128,2048]{1,0:T(8,128)(2,1)S(1)}, u32[]{:S(2)}, u32[]{:S(2)}) collective-permute-start(bf16[128,2048]{1,0:T(8,128)(2,1)S(1)} %get-tuple-element.50), channel_id=1, source_target_pairs={{0,24},{8,0},{16,8},{24,16},{1,25},{9,1},{17,9},{25,17},{2,26},{10... | collective-permute-start | bytes 1572872 | tf_op jit(solution)/shard_map/ppermute | solution.py:43
  79.1 14.8 %collective-permute-start.30 = (bf16[128,2048]{1,0:T(8,128)(2,1)S(1)}, bf16[128,2048]{1,0:T(8,128)(2,1)S(1)}, u32[]{:S(2)}, u32[]{:S(2)}) collective-permute-start(bf16[128,2048]{1,0:T(8,128)(2,1)S(1)} %get-tuple-element.47.refs_4_.refs_6_), channel_id=1, source_target_pairs={{0,4},{4,0},{2,6},{6,2},{1,5},{5,1},{3,7},{7,3},{8,12},{12,8},{10,... | collective-permute-start | bytes 1572872 | tf_op jit(solution)/shard_map/ppermute | solution.py:74
  80.4 14.8 %collective-permute-start.21 = (bf16[128,2048]{1,0:T(8,128)(2,1)S(1)}, bf16[128,2048]{1,0:T(8,128)(2,1)S(1)}, u32[]{:S(2)}, u32[]{:S(2)}) collective-permute-start(bf16[128,2048]{1,0:T(8,128)(2,1)S(1)} %collective-permute-done.3.got_ref.refs_4_.refs_6_), channel_id=1, source_target_pairs={{0,2},{2,0},{4,6},{6,4},{1,3},{3,1},{5,7},{7,5},{8,10},{10,8},{12,... | collective-permute-start | bytes 1572872 | tf_op jit(solution)/shard_map/ppermute | solution.py:74
  82.9 20.0 %collective-permute-start.32 = (bf16[128,2048]{1,0:T(8,128)(2,1)S(1)}, bf16[128,2048]{1,0:T(8,128)(2,1)S(1)}, u32[]{:S(2)}, u32[]{:S(2)}) collective-permute-start(bf16[128,2048]{1,0:T(8,128)(2,1)S(1)} %get-tuple-element.52.refs_4_.refs_7_), channel_id=1, source_target_pairs={{0,4},{4,0},{2,6},{6,2},{1,5},{5,1},{3,7},{7,3},{8,12},{12,8},{10,... | collective-permute-start | bytes 1572872 | tf_op jit(solution)/shard_map/ppermute | solution.py:74
  84.6 20.7 %collective-permute-start.23 = (bf16[128,2048]{1,0:T(8,128)(2,1)S(1)}, bf16[128,2048]{1,0:T(8,128)(2,1)S(1)}, u32[]{:S(2)}, u32[]{:S(2)}) collective-permute-start(bf16[128,2048]{1,0:T(8,128)(2,1)S(1)} %collective-permute-done.12.got_ref.refs_4_.refs_7_), channel_id=1, source_target_pairs={{0,2},{2,0},{4,6},{6,4},{1,3},{3,1},{5,7},{7,5},{8,10},{10,8},{12,... | collective-permute-start | bytes 1572872 | tf_op jit(solution)/shard_map/ppermute | solution.py:74
  86.7 16.7 %collective-permute-start.29 = (bf16[512,384]{1,0:T(8,128)(2,1)S(1)}, bf16[512,384]{1,0:T(8,128)(2,1)S(1)}, u32[]{:S(2)}, u32[]{:S(2)}) collective-permute-start(bf16[512,384]{1,0:T(8,128)(2,1)S(1)} %shard_map.134.refs_3_), channel_id=1, source_target_pairs={{0,1},{1,0},{2,3},{3,2},{4,5},{5,4},{6,7},{7,6},{8,9},{9,8},{10,11... | collective-permute-start | bytes 1179656 | tf_op jit(solution)/shard_map/ppermute | solution.py:51
  93.9 13.3 %collective-permute-start.20 = (bf16[512,384]{1,0:T(8,128)(2,1)S(1)}, bf16[512,384]{1,0:T(8,128)(2,1)S(1)}, u32[]{:S(2)}, u32[]{:S(2)}) collective-permute-start(bf16[512,384]{1,0:T(8,128)(2,1)S(1)} %shard_map.130.refs_3_), channel_id=1, source_target_pairs={{0,1},{1,0},{2,3},{3,2},{4,5},{5,4},{6,7},{7,6},{8,9},{9,8},{10,11... | collective-permute-start | bytes 1179656 | tf_op jit(solution)/shard_map/ppermute | solution.py:51
  98.5 10.1 %collective-permute-start.31 = (bf16[128,256]{1,0:T(8,128)(2,1)S(1)}, bf16[128,256]{1,0:T(8,128)(2,1)S(1)}, u32[]{:S(2)}, u32[]{:S(2)}) collective-permute-start(bf16[128,256]{1,0:T(8,128)(2,1)S(1)} %shard_map.135.refs_5_), channel_id=1, source_target_pairs={{0,1},{1,0},{2,3},{3,2},{4,5},{5,4},{6,7},{7,6},{8,9},{9,8},{10,11... | collective-permute-start | bytes 196616 | tf_op jit(solution)/shard_map/ppermute | solution.py:51
  102.9 9.3 %collective-permute-start.22 = (bf16[128,256]{1,0:T(8,128)(2,1)S(1)}, bf16[128,256]{1,0:T(8,128)(2,1)S(1)}, u32[]{:S(2)}, u32[]{:S(2)}) collective-permute-start(bf16[128,256]{1,0:T(8,128)(2,1)S(1)} %shard_map.131.refs_5_), channel_id=1, source_target_pairs={{0,1},{1,0},{2,3},{3,2},{4,5},{5,4},{6,7},{7,6},{8,9},{9,8},{10,11... | collective-permute-start | bytes 196616 | tf_op jit(solution)/shard_map/ppermute | solution.py:51
  103.4 6.8 %collective-permute-start.33 = (bf16[128,256]{1,0:T(8,128)(2,1)S(1)}, bf16[128,256]{1,0:T(8,128)(2,1)S(1)}, u32[]{:S(2)}, u32[]{:S(2)}) collective-permute-start(bf16[128,256]{1,0:T(8,128)(2,1)S(1)} %shard_map.136.refs_7_), channel_id=1, source_target_pairs={{0,1},{1,0},{2,3},{3,2},{4,5},{5,4},{6,7},{7,6},{8,9},{9,8},{10,11... | collective-permute-start | bytes 196616 | tf_op jit(solution)/shard_map/ppermute | solution.py:51
  105.3 14.9 %collective-permute-start.36 = (bf16[128,2048]{1,0:T(8,128)(2,1)S(1)}, bf16[128,2048]{1,0:T(8,128)(2,1)S(1)}, u32[]{:S(2)}, u32[]{:S(2)}) collective-permute-start(bf16[128,2048]{1,0:T(8,128)(2,1)S(1)} %get-tuple-element.65), channel_id=1, source_target_pairs={{0,2},{4,6},{2,0},{6,4},{1,3},{5,7},{3,1},{7,5},{8,10},{12,14},{10... | collective-permute-start | bytes 1572872 | tf_op jit(solution)/shard_map/ppermute | solution.py:82
  108.6 14.9 %collective-permute-start.35 = (bf16[128,2048]{1,0:T(8,128)(2,1)S(1)}, bf16[128,2048]{1,0:T(8,128)(2,1)S(1)}, u32[]{:S(2)}, u32[]{:S(2)}) collective-permute-start(bf16[128,2048]{1,0:T(8,128)(2,1)S(1)} %get-tuple-element.63), channel_id=1, source_target_pairs={{0,4},{2,6},{4,0},{6,2},{1,5},{3,7},{5,1},{7,3},{8,12},{10,14},{12... | collective-permute-start | bytes 1572872 | tf_op jit(solution)/shard_map/ppermute | solution.py:82
  111.6 18.8 %collective-permute-start.34 = (bf16[128,2048]{1,0:T(8,128)(2,1)S(1)}, bf16[128,2048]{1,0:T(8,128)(2,1)S(1)}, u32[]{:S(2)}, u32[]{:S(2)}) collective-permute-start(bf16[128,2048]{1,0:T(8,128)(2,1)S(1)} %get-tuple-element.61), channel_id=1, source_target_pairs={{0,2},{4,6},{2,0},{6,4},{1,3},{5,7},{3,1},{7,5},{8,10},{12,14},{10... | collective-permute-start | bytes 1572872 | tf_op jit(solution)/shard_map/ppermute | solution.py:82
  113.6 20.6 %collective-permute-start.25 = (bf16[128,2048]{1,0:T(8,128)(2,1)S(1)}, bf16[128,2048]{1,0:T(8,128)(2,1)S(1)}, u32[]{:S(2)}, u32[]{:S(2)}) collective-permute-start(bf16[128,2048]{1,0:T(8,128)(2,1)S(1)} %get-tuple-element.56), channel_id=1, source_target_pairs={{0,4},{2,6},{4,0},{6,2},{1,5},{3,7},{5,1},{7,3},{8,12},{10,14},{12... | collective-permute-start | bytes 1572872 | tf_op jit(solution)/shard_map/ppermute | solution.py:82
  (19 other events, 70.9 us)
where the time goes:
time: 136 us
  waiting for transfers between devices  66.7 us (49%)
  Pallas kernels  35.1 us (26%)
  starting transfers between devices  31.4 us (23%)
  local copies, waits for them, and re-layouts  1.44 us (1%)
    ppermute x10, waiting for transfers between devices, to_partner(): return lax.ppermute(x, 'dp', pairs)  41.5 us
    pallas_call x30, Pallas kernels, call(): pl.pallas_call(kernel, out_shape=outs, in_specs=specs or [VMEM] * len(ope...  35.1 us
    ppermute x4, waiting for transfers between devices, to_group(): return lax.ppermute(x, 'dp', pairs)  18.4 us
    ppermute x10, starting transfers between devices, to_partner(): return lax.ppermute(x, 'dp', pairs)  10.6 us
    ppermute x19, starting transfers between devices, with_peers(): parts.append(lax.ppermute(part, axis, [(i, to(i)) for i in range(count)]))  7.76 us
    ppermute x2, starting transfers between devices, moved_by(): return lax.ppermute(x, axis, [(i, (i + by) % count) for i in range(count)])  6.16 us
    ppermute x2, waiting for transfers between devices, moved_by(): return lax.ppermute(x, axis, [(i, (i + by) % count) for i in range(count)])  4.41 us
    ppermute x4, starting transfers between devices, to_group(): return lax.ppermute(x, 'dp', pairs)  4.31 us
  transfers between devices with their start and end apart: 37, of which 17 were waited for; matrix products, arithmetic and copies ran while one was open for 0% of the time, Pallas kernels for 22%

commit v1 on v0

--- a/solution.py
+++ b/solution.py
@@ -10,6 +10,7 @@
 
 EPS = 1e-05
 LANES = 128
+PIPE, DP, TENSOR = "pipe", "dp", "tensor"
 START_LIMIT = 46<<20
 
 
@@ -54,12 +55,12 @@
 
 class Pairing:
     def __init__(self, lowest):
-        self.count = lax.axis_size("dp")
+        self.count = lax.axis_size(DP)
         self.groups = self.count // 2
         self.lowest = lowest
 
     def place(self):
-        me = lax.axis_index("dp")
+        me = lax.axis_index(DP)
         if self.lowest:
             return lax.rem(me, 2), me // 2
         return me // self.groups, lax.rem(me, self.groups)
@@ -71,7 +72,7 @@
         pairs = [
             (self.index(g, b), self.index(g, 1 - b)) for g in range(self.groups) for b in range(2)
         ]
-        return lax.ppermute(x, "dp", pairs)
+        return lax.ppermute(x, DP, pairs)
 
     def to_group(self, x, by):
         pairs = [
@@ -79,7 +80,7 @@
             for g in range(self.groups)
             for b in range(2)
         ]
-        return lax.ppermute(x, "dp", pairs)
+        return lax.ppermute(x, DP, pairs)
 
     def starts(self, b, piece):
         return [pl.multiple_of(self.index(g, b) * piece, piece) for g in range(self.groups)]
@@ -88,6 +89,12 @@
 def tiles_of(width):
     tile = 512 if width % 512 == 0 else LANES
     return [slice(at, at + tile) for at in range(0, width, tile)]
+
+
+def columns_of(refs, cut):
+    part = refs[0].shape[1]
+    which = cut.start // part
+    return refs[which][:, cut.start - which * part : cut.stop - which * part]
 
 
 def pre_rows(saved, v, weight_of, gain_ref):
@@ -137,22 +144,35 @@
     out_ref[:, rank:] = squares
 
 
-def upper_kernel(sections, t, got_ref, entering_ref, wout_ref, cot_ref, part_ref):
-    is_top = lax.axis_index("pipe") == sections - 1
+def upper_kernel(sections, t, got_ref, entering_ref, wout_ref, *refs):
+    cot_refs, part_ref = refs[:-1], refs[-1]
+    is_top = lax.axis_index(PIPE) == sections - 1
+    width = cot_refs[0].shape[1]
 
     @pl.when(is_top)
     def _():
-        cot_ref[...] = entering_ref[t]
+        for i, ref in enumerate(cot_refs):
+            ref[...] = entering_ref[t, :, i * width : (i + 1) * width]
 
     @pl.when(jnp.logical_not(is_top))
     def _():
-        cot_ref[...] = got_ref[...]
-
-    part_ref[...] = dot(cot_ref[...], wout_ref[...], ((1,), (1,))).astype(jnp.bfloat16)
-
-
-def lower_kernel(got_ref, wout_ref, part_ref):
-    part_ref[...] = dot(got_ref[...], wout_ref[...], ((1,), (1,))).astype(jnp.bfloat16)
+        for i, ref in enumerate(cot_refs):
+            ref[...] = got_ref[:, i * width : (i + 1) * width]
+
+    total = None
+    for cut in tiles_of(wout_ref.shape[1]):
+        term = dot(columns_of(cot_refs, cut), wout_ref[:, cut], ((1,), (1,)))
+        total = term if total is None else total + term
+    part_ref[...] = total.astype(jnp.bfloat16)
+
+
+def lower_kernel(*refs):
+    wout_ref, part_ref = refs[-2:]
+    total = None
+    for cut in tiles_of(wout_ref.shape[1]):
+        term = dot(columns_of(refs[:-2], cut), wout_ref[:, cut], ((1,), (1,)))
+        total = term if total is None else total + term
+    part_ref[...] = total.astype(jnp.bfloat16)
 
 
 def half_weight(ref, pairing, cut):
@@ -177,9 +197,13 @@
     out_ref[place, half:] = jnp.zeros((rows, LANES), jnp.bfloat16)
 
 
-def partner_back_kernel(pairing, cot_ref, wout_ref, out_ref):
-    weight = half_weight(wout_ref, pairing, slice(0, cot_ref.shape[1]))
-    out_ref[...] = dot(cot_ref[...], weight, ((1,), (1,))).astype(jnp.bfloat16)
+def partner_back_kernel(pairing, *refs):
+    wout_ref, out_ref = refs[-2:]
+    total = None
+    for cut in tiles_of(wout_ref.shape[1]):
+        term = dot(columns_of(refs[:-2], cut), half_weight(wout_ref, pairing, cut), ((1,), (1,)))
+        total = term if total is None else total + term
+    out_ref[...] = total.astype(jnp.bfloat16)
 
 
 def summed(parts, where, columns):
@@ -202,12 +226,13 @@
     return sigma * (1.0 + pre * (1.0 - sigma))
 
 
-def step_kernel(v, saved_at, at, back_at, peers, full_width, pairing, mode, *refs):
+def step_kernel(v, saved_at, at, back_at, peers, full_width, pairing, mode, cot_parts, out_parts, *refs):
     firsts, backs, refs = refs[:peers], refs[peers : 2 * peers], refs[2 * peers :]
-    cot_ref, saved_ref, win_ref, gain_ref, refs = *refs[:4], refs[4:]
+    cot_refs, refs = refs[:cot_parts], refs[cot_parts:]
+    saved_ref, win_ref, gain_ref, refs = *refs[:3], refs[3:]
     if mode != "plain":
         other_ref, refs = refs[0], refs[1:]
-    out_ref, mine_ref, turned = refs
+    out_refs, (mine_ref, turned) = refs[:out_parts], refs[out_parts:]
     rows, width = saved_ref.shape[1:]
     rank = win_ref.shape[0]
     where = slice(at * rows, (at + 1) * rows)
@@ -221,20 +246,24 @@
 
     for cut in tiles_of(width):
         result = (
-            cot_ref[:, cut].astype(jnp.float32)
+            columns_of(cot_refs, cut).astype(jnp.float32)
             + gain_ref[v, :, cut] * dot(scaled, win_ref[:, cut], ((1,), (0,)))
             - saved_ref[saved_at, :, cut].astype(jnp.float32) * pull
         ).astype(jnp.bfloat16)
         if mode == "both":
-            out_ref[0, :, cut] = result
-            out_ref[1, :, cut] = other_ref[:, cut]
+            out_refs[0][0, :, cut] = result
+            out_refs[0][1, :, cut] = other_ref[:, cut]
         else:
-            out_ref[:, cut] = result
+            part = width // out_parts
+            which = cut.start // part
+            out_refs[which][:, cut.start - which * part : cut.stop - which * part] = result
     if mode == "bottom":
 
-        @pl.when(lax.axis_index("pipe") == 0)
+        @pl.when(lax.axis_index(PIPE) == 0)
         def _():
-            out_ref[...] = other_ref[...]
+            part = width // out_parts
+            for which, ref in enumerate(out_refs):
+                ref[...] = other_ref[:, which * part : (which + 1) * part]
 
     b, _ = pairing.place()
     piece = rank // pairing.count
@@ -244,7 +273,7 @@
             mine_ref[k, g * piece : (g + 1) * piece] = turned[k, pl.ds(start, piece)]
 
 
-def grad_kernel(k, v, steps, peers, full_width, pairing, operands, *refs):
+def grad_kernel(k, v, steps, peers, full_width, pairing, base, rights, *refs):
     mine, refs = refs[:steps], refs[steps:]
     firsts, refs = refs[:peers], refs[peers:]
     backs = [[firsts, steps]]
@@ -252,7 +281,7 @@
         for _ in range(1, steps):
             backs.append([refs[:peers], 0])
             refs = refs[peers:]
-    rights, refs = refs[:operands], refs[operands:]
+    rights, refs = refs[:rights], refs[rights:]
     own_ref, sends, turned = refs[0], refs[1:-1], refs[-1]
     half, rows = mine[0].shape[1:]
     for t in range(steps):
@@ -276,15 +305,16 @@
             chunks.append(jnp.concatenate([mine[t][k, at], turned[t, at]], axis=1))
         lefts.append(jnp.concatenate(chunks, axis=0))
     for cut in tiles_of(width):
+        place = slice(base + cut.start, base + cut.stop)
         total = None
         for t in range(steps):
             if k:
-                pair = [rights[t][:, cut], rights[steps + t][:, cut]]
+                pair = [ref[:, cut if ref.shape[1] == width else place] for ref in (rights[t], rights[steps + t])]
             else:
-                gain = rights[4][v, :, cut]
-                refs_at = ((rights[1], t - 1), (rights[3], t - 1)) if t else ((rights[0], 0), (rights[2], 0))
+                gain = rights[4][v, :, place]
+                refs_at = [(rights[i + min(t, 1)], max(t - 1, 0)) for i in (0, 2)]
                 pair = [
-                    (ref[at, :, cut].astype(jnp.float32) * gain).astype(jnp.bfloat16) for ref, at in refs_at
+                    (ref[at, :, place].astype(jnp.float32) * gain).astype(jnp.bfloat16) for ref, at in refs_at
                 ]
             term = dot(lefts[t], jnp.concatenate(pair, axis=0), ((1,), (0,)))
             total = term if total is None else total + term
@@ -301,6 +331,21 @@
         for ref in parts[1:]:
             total = total + ref[...].astype(jnp.float32)
         out_ref[v] = total * scale
+
+
+def final(scale, count, parts, whole, at, before):
+    operands = tuple(parts) + (() if before is None else (before,))
+    share = parts[0].shape[1]
+    return pl.pallas_call(
+        functools.partial(final_kernel, scale, count),
+        grid=(1,),
+        out_shape=whole,
+        in_specs=[VMEM] * len(parts) + [pl.BlockSpec(memory_space=pl.ANY)] * (len(operands) - len(parts)),
+        out_specs=pl.BlockSpec((2, whole.shape[1], share), lambda _: (0, 0, at)),
+        input_output_aliases={} if before is None else {len(parts): 0},
+        compiler_params=pltpu.CompilerParams(vmem_limit_bytes=8 << 20),
+        cost_estimate=pl.CostEstimate(flops=whole.size * 16, bytes_accessed=0, transcendentals=0),
+    )(*operands)
 
 
 def stats_kernel(rewards_ref, ids_ref, out_ref):
@@ -343,9 +388,9 @@
 def shards(
     saved_inputs, proj_in, proj_out, norm_gain, arriving, logp_grad, rewards, seq_lengths, group_ids
 ):
-    sections = lax.axis_size("pipe")
-    replicas = lax.axis_size("dp")
-    peers = lax.axis_size("tensor")
+    sections = lax.axis_size(PIPE)
+    replicas = lax.axis_size(DP)
+    peers = lax.axis_size(TENSOR)
     first_cots = [arriving[v, 0] for v in range(2)]
     later_saved = [saved_inputs[1:, v, 0] for v in range(2)]
     steps, rows, width = saved_inputs.shape[0], *later_saved[0].shape[1:]
@@ -361,17 +406,20 @@
     def partner(v, x):
         return pairings[v].to_partner(x)
 
+    def exchanged(v, parts):
+        return tuple(partner(v, part) for part in parts)
+
     stats = call(stats_kernel, shape((8, LANES), f32), (rewards, group_ids), 1000, specs=[SMEM, SMEM])
     entering = call(
         functools.partial(entering_kernel, replicas),
         shape((new_count, rows, width), bf16),
-        (rewards, group_ids, seq_lengths, logp_grad, *with_peers(stats, "dp")),
+        (rewards, group_ids, seq_lengths, logp_grad, *with_peers(stats, DP)),
         product // 4,
         specs=[SMEM] * 3 + [VMEM] * (1 + replicas),
     )
 
-    cots = [first_cots]
-    theirs_c = [[partner(v, first_cots[v]) for v in range(2)]]
+    cots = [[(cot,) for cot in first_cots]]
+    theirs_c = [[exchanged(v, cots[0][v]) for v in range(2)]]
 
     firsts, laters, w_in, w_out = [None] * 2, [[None], [None]], [None] * 2, [None] * 2
     for v in (1, 0):
@@ -389,7 +437,7 @@
         )
         if v:
             first_saved = tokens[::-1]
-        firsts[v] = with_peers(part, "tensor")
+        firsts[v] = with_peers(part, TENSOR)
     theirs_first = [partner(v, first_saved[v]) for v in range(2)]
     theirs_later = [partner(v, later_saved[v]) for v in range(2)]
     for t in range(1, steps):
@@ -400,21 +448,26 @@
                 (later_saved[v], w_in[v], norm_gain),
                 product,
             )
-            laters[v].append(with_peers(part, "tensor"))
+            laters[v].append(with_peers(part, TENSOR))
 
     def finish(v, t, backs, mode, other):
-        operands = (*(laters[v][t] if t else firsts[v]), *backs, cots[t][v])
+        operands = (*(laters[v][t] if t else firsts[v]), *backs, *cots[t][v])
         operands += (later_saved[v] if t else first_saved[v], w_in[v], norm_gain)
         if mode != "plain":
             operands = operands + (other,)
         at, back_at = max(t - 1, 0), 0 if t else 1
-        return call(
-            functools.partial(step_kernel, v, at, 0, back_at, peers, full_width, pairings[v], mode),
-            [shape((2, rows, width) if mode == "both" else (rows, width), bf16), shape((2, half, rows), bf16)],
+        parts = 1 if v else cot_parts(t + 1, steps)
+        *out, side = call(
+            functools.partial(
+                step_kernel, v, at, 0, back_at, peers, full_width, pairings[v], mode, len(cots[t][v]), parts
+            ),
+            [shape((2, rows, width) if mode == "both" else (rows, width // parts), bf16)] * parts
+            + [shape((2, half, rows), bf16)],
             operands,
             product,
             scratch=[pltpu.VMEM((2, rank, rows), bf16)],
         )
+        return tuple(out), side
 
     mine, backs = [], firsts
     line = [(s, s - 1) for s in range(1, sections)]
@@ -423,72 +476,88 @@
         last = t + 1 == steps
         for v in (1, 0):
             mode = "plain" if v else ("both" if last else "bottom")
-            now[v], side[v] = finish(v, t, backs[v], mode, now[1])
+            now[v], side[v] = finish(v, t, backs[v], mode, None if v else now[1][0])
         mine.append(side)
         if last:
-            leaving = now[0]
+            leaving = now[0][0]
             break
-        upper = lax.ppermute(now[1], "pipe", line)
-        lower = moved_by(now[0], "pipe", -1)
-        cot_upper, part = call(
+        upper = lax.ppermute(now[1][0], PIPE, line)
+        lower = tuple(moved_by(part, PIPE, -1) for part in now[0])
+        parts = cot_parts(t + 1, steps)
+        *cot_upper, part = call(
             functools.partial(upper_kernel, sections, t),
-            [shape((rows, width), bf16), shape((rows, rank), bf16)],
+            [shape((rows, width // parts), bf16)] * parts + [shape((rows, rank), bf16)],
             (upper, entering, w_out[1]),
             product,
         )
-        backs = [None, with_peers(part, "tensor")]
-        part = call(lower_kernel, shape((rows, rank), bf16), (lower, w_out[0]), product)
-        backs[0] = with_peers(part, "tensor")
-        cots.append([lower, cot_upper])
-        theirs_c.append([partner(v, cots[t + 1][v]) for v in range(2)])
+        backs = [None, with_peers(part, TENSOR)]
+        part = call(lower_kernel, shape((rows, rank), bf16), (*lower, w_out[0]), product)
+        backs[0] = with_peers(part, TENSOR)
+        cots.append([lower, tuple(cot_upper)])
+        theirs_c.append([exchanged(v, cots[t + 1][v]) for v in range(2)])
 
     peer_firsts, peer_backs = [None, None], [[], []]
     for v in (1, 0):
         part = call(
             functools.partial(partner_kernel, v, pairings[v]),
             shape(((steps + 1) * rows, half + LANES), bf16),
-            (theirs_first[v], theirs_later[v], theirs_c[0][v], w_in[v], w_out[v], norm_gain),
+            (theirs_first[v], theirs_later[v], theirs_c[0][v][0], w_in[v], w_out[v], norm_gain),
             (steps + 1) * product // 2,
         )
-        peer_firsts[v] = with_peers(part, "tensor")
+        peer_firsts[v] = with_peers(part, TENSOR)
         for t in range(1, steps):
             part = call(
                 functools.partial(partner_back_kernel, pairings[v]),
                 shape((rows, half), bf16),
-                (theirs_c[t][v], w_out[v]),
+                (*theirs_c[t][v], w_out[v]),
                 product // 2,
             )
-            peer_backs[v] += with_peers(part, "tensor")
+            peer_backs[v] += with_peers(part, TENSOR)
 
     scale = 1.0 / (replicas * rows)
     grads = []
     for k in (0, 1):
-        parts = []
+        splits = cot_parts(steps - 1, steps)
+        parts = [[] for _ in range(splits)]
         for v in range(2):
             if k:
-                rights = tuple(cots[t][v] for t in range(steps)) + tuple(theirs_c[t][v] for t in range(steps))
+                groups = [cots[t][v] for t in range(steps)] + [theirs_c[t][v] for t in range(steps)]
+                given = ()
             else:
-                rights = tuple(peer_backs[v])
-                rights += (first_saved[v], later_saved[v], theirs_first[v], theirs_later[v], norm_gain)
-            own, *sends = call(
-                functools.partial(
-                    grad_kernel, k, v, steps, peers, full_width, pairings[v], 2 * steps if k else 5
-                ),
-                [shape((piece, width), f32)] + [shape((piece, width), bf16)] * (pairings[v].groups - 1),
-                tuple(mine[t][v] for t in range(steps)) + tuple(peer_firsts[v]) + rights,
-                steps * product,
-                scratch=[pltpu.VMEM((steps, half, rows), bf16)],
-            )
-            parts += [own] + [pairings[v].to_group(send, by + 1) for by, send in enumerate(sends)]
-        grads.append(
-            call(
-                functools.partial(final_kernel, scale, len(parts) // 2),
-                shape((2, piece, width), f32),
-                tuple(parts),
-                product // 8,
-            )
-        )
+                groups = [(x,) for x in (first_saved[v], later_saved[v], theirs_first[v], theirs_later[v], norm_gain)]
+                given = tuple(peer_backs[v])
+            for i in range(splits):
+                share = width // splits
+                own, *sends = call(
+                    functools.partial(
+                        grad_kernel,
+                        k,
+                        v,
+                        steps,
+                        peers,
+                        full_width,
+                        pairings[v],
+                        i * share,
+                        len(groups),
+                    ),
+                    [shape((piece, share), f32)] + [shape((piece, share), bf16)] * (pairings[v].groups - 1),
+                    tuple(mine[t][v] for t in range(steps))
+                    + tuple(peer_firsts[v])
+                    + given
+                    + tuple(group[i if len(group) == splits else 0] for group in groups),
+                    steps * product // splits,
+                    scratch=[pltpu.VMEM((steps, half, rows), bf16)],
+                )
+                parts[i] += [own] + [pairings[v].to_group(send, by + 1) for by, send in enumerate(sends)]
+        total = None
+        for i in range(splits):
+            total = final(scale, len(parts[i]) // 2, parts[i], shape((2, piece, width), f32), i, total)
+        grads.append(total)
     return (grads[0][:, None], grads[1][:, None], leaving[:, None])
+
+
+def cot_parts(t, steps):
+    return 2 if t + 1 == steps else 1
 
 
 def solution(mesh):
@@ -496,20 +565,20 @@
         shards,
         mesh=mesh,
         in_specs=(
-            P(None, None, "pipe", "dp", "tensor"),
-            P(None, "pipe", None, "tensor"),
-            P(None, "pipe", None, "tensor"),
-            P(None, "pipe", "tensor"),
-            P(None, "pipe", "dp", "tensor"),
-            P(None, "dp", "tensor"),
-            P(None, "dp", None),
-            P(None, "dp", None),
-            P(None, "dp", None),
+            P(None, None, PIPE, DP, TENSOR),
+            P(None, PIPE, None, TENSOR),
+            P(None, PIPE, None, TENSOR),
+            P(None, PIPE, TENSOR),
+            P(None, PIPE, DP, TENSOR),
+            P(None, DP, TENSOR),
+            P(None, DP, None),
+            P(None, DP, None),
+            P(None, DP, None),
         ),
         out_specs=(
-            P(None, "pipe", "dp", "tensor"),
-            P(None, "pipe", "dp", "tensor"),
-            P(None, "pipe", "dp", "tensor"),
+            P(None, PIPE, DP, TENSOR),
+            P(None, PIPE, DP, TENSOR),
+            P(None, PIPE, DP, TENSOR),
         ),
         check_vma=False,
     )

time: 136 us -> 141 us (1.037)
  starting transfers between devices: 31.4 us -> 42.6 us
  waiting for transfers between devices: 66.7 us -> 57.8 us
  Pallas kernels: 35.1 us -> 38.1 us
    ppermute x16 -> x22, starting transfers between devices: 17.5 us -> 25.7 us  [the longest x12 12.6 us: to_partner(): return lax.ppermute(x, DP, pairs)]
    ppermute x16 -> x22, waiting for transfers between devices: 59.8 us -> 51.8 us  [the longest x12 42.9 us: to_partner(): return lax.ppermute(x, DP, pairs)]
    pallas_call x0 -> x4, Pallas kernels: none -> 4.29 us  [final(): pl.pallas_call(functools.partial(final_kernel, scale, count), grid=(1,),...]
    ppermute x2 -> x3, starting transfers between devices: 6.16 us -> 8.77 us  [moved_by(): return lax.ppermute(x, axis, [(i, (i + by) % count) for i in range(count)])]
    pallas_call x30 -> x32, Pallas kernels: 35.1 us -> 33.8 us  [call(): pl.pallas_call(kernel, out_shape=outs, in_specs=specs or [VMEM] * len(ope...]
    ppermute x2 -> x3, waiting for transfers between devices: 4.41 us -> 3.67 us  [moved_by(): return lax.ppermute(x, axis, [(i, (i + by) % count) for i in range(count)])]
  transfers between devices with their start and end apart: 37 -> 44, of which waited for: 17 -> 16; matrix products, arithmetic and copies ran while one was open for 0% -> 0% of each run, Pallas kernels for 22% -> 24%
where the time goes in v1:
time: 141 us
  waiting for transfers between devices  57.8 us (41%)
  starting transfers between devices  42.6 us (30%)
  Pallas kernels  38.1 us (27%)
  local copies, waits for them, and re-layouts  1.55 us (1%)
    ppermute x12, waiting for transfers between devices, to_partner(): return lax.ppermute(x, DP, pairs)  42.9 us
    pallas_call x32, Pallas kernels, call(): pl.pallas_call(kernel, out_shape=outs, in_specs=specs or [VMEM] * len(ope...  33.8 us
    ppermute x12, starting transfers between devices, to_partner(): return lax.ppermute(x, DP, pairs)  12.6 us
    ppermute x8, starting transfers between devices, to_group(): return lax.ppermute(x, DP, pairs)  10.3 us
    ppermute x8, waiting for transfers between devices, to_group(): return lax.ppermute(x, DP, pairs)  8.87 us
    ppermute x3, starting transfers between devices, moved_by(): return lax.ppermute(x, axis, [(i, (i + by) % count) for i in range(count)])  8.77 us
    ppermute x19, starting transfers between devices, with_peers(): parts.append(lax.ppermute(part, axis, [(i, to(i)) for i in range(count)]))  8.14 us
    pallas_call x4, Pallas kernels, final(): pl.pallas_call(functools.partial(final_kernel, scale, count), grid=(1,),...  4.29 us
  transfers between devices with their start and end apart: 44, of which 16 were waited for; matrix products, arithmetic and copies ran while one was open for 0% of the time, Pallas kernels for 24%

profile of v1, /device:TPU:0, one launch (start us, length us, event | category | flops | bytes accessed | tf_op | source)
XLA Modules:
  0.0 141.2 jit_solution(17121459970719135421)
XLA Ops:
  1.9 3.4 %shard_map.112 = (bf16[256,640]{1,0:T(8,128)(2,1)S(1)}, bf16[512,2048]{1,0:T(8,128)(2,1)S(1)}, bf16[512,2048]{1,0:T(8,128)(2,1)S(1)}, bf16[1,128,2048]{2,1,0:T(8,128)(2,1)S(1)}, bf16[1,128,2048]{2,1,0:T(8,128)(2,1)S(1)}) custom-call(bf16[3,2,1,128,2048]{4,3,2,1,0:T(8,128)(2,1)} %saved_ref.3, bf16[2,1,512,2048]{3,2,1,0:T(8,128)(2,1)} %proj_in_ref.3, ...), custom_call_target="tpu_custom_call" | custom-call | flops 536870912 | tf_op jit(solution)/shard_map/pallas_call | solution.py:23
  5.9 3.3 %shard_map.113 = (bf16[256,640]{1,0:T(8,128)(2,1)S(1)}, bf16[512,2048]{1,0:T(8,128)(2,1)S(1)}, bf16[512,2048]{1,0:T(8,128)(2,1)S(1)}) custom-call(bf16[3,2,1,128,2048]{4,3,2,1,0:T(8,128)(2,1)} %saved_ref.3, bf16[2,1,512,2048]{3,2,1,0:T(8,128)(2,1)} %proj_in_ref.3, bf16[2,1,512,2048]{3,2,1,0:T(8,128)(2,1)} %proj_out_ref.3, f32[2,1,2048]{2,1,0:T(1,128)S(1)} %copy-done, ...), custom_call_target="tpu_custom_call" | custom-call | flops 536870912 | tf_op jit(solution)/shard_map/pallas_call | solution.py:23
  12.4 6.2 %collective-permute-start.3 = (bf16[128,2048]{1,0:T(8,128)(2,1)S(1)}, bf16[128,2048]{1,0:T(8,128)(2,1)S(1)}, u32[]{:S(2)}, u32[]{:S(2)}) collective-permute-start(bf16[128,2048]{1,0:T(8,128)(2,1)S(1)} %get-tuple-element.53), channel_id=1, source_target_pairs={{0,24},{8,0},{16,8},{24,16},{1,25},{9,1},{17,9},{25,17},{2,26},{10... | collective-permute-start | bytes 1572872 | tf_op jit(solution)/shard_map/ppermute | solution.py:44
  20.4 2.5 %collective-permute-start.9 = (f32[8,128]{1,0:T(8,128)S(1)}, f32[8,128]{1,0:T(8,128)S(1)}, u32[]{:S(2)}, u32[]{:S(2)}) collective-permute-start(f32[8,128]{1,0:T(8,128)S(1)} %shard_map.119.refs_0_), channel_id=1, source_target_pairs={{0,6},{2,4},{4,2},{6,0},{1,7},{3,5},{5,3},{7,1},{8,14},{10,12},{12... | collective-permute-start | bytes 12296 | tf_op jit(solution)/shard_map/ppermute | solution.py:52
  33.5 1.6 %collective-permute-start.20 = (bf16[128,2048]{1,0:T(8,128)(2,1)S(1)}, bf16[128,2048]{1,0:T(8,128)(2,1)S(1)}, u32[]{:S(2)}, u32[]{:S(2)}) collective-permute-start(bf16[128,2048]{1,0:T(8,128)(2,1)S(1)} %get-tuple-element.93.cot_ref.refs_4_.refs_5_), channel_id=1, source_target_pairs={{0,2},{2,0},{4,6},{6,4},{1,3},{3,1},{5,7},{7,5},{8,10},{10,8},{12,... | collective-permute-start | bytes 1572872 | tf_op jit(solution)/shard_map/ppermute | solution.py:75
  35.1 3.3 %collective-permute-done.3.refs_0_.refs_4_.refs_6_ = bf16[128,2048]{1,0:T(8,128)(2,1)S(1)} collective-permute-done((bf16[128,2048]{1,0:T(8,128)(2,1)S(1)}, bf16[128,2048]{1,0:T(8,128)(2,1)S(1)}, u32[]{:S(2)}, u32[]{:S(2)}) %collective-permute-start.3) | collective-permute-done | bytes 524320 | tf_op jit(solution)/shard_map/ppermute | solution.py:44
  39.8 1.7 %collective-permute-start.28 = (bf16[1,128,2048]{2,1,0:T(8,128)(2,1)S(1)}, bf16[1,128,2048]{2,1,0:T(8,128)(2,1)S(1)}, u32[]{:S(2)}, u32[]{:S(2)}) collective-permute-start(bf16[1,128,2048]{2,1,0:T(8,128)(2,1)S(1)} %get-tuple-element.49.refs_5_.refs_9_), channel_id=1, source_target_pairs={{0,4},{4,0},{2,6},{6,2},{1,5},{5,1},{3,7},{7,3},{8,12},{12,8},{10,... | collective-permute-start | bytes 1572872 | tf_op jit(solution)/shard_map/ppermute | solution.py:75
  41.8 1.7 %collective-permute-start.19 = (bf16[2,128,2048]{2,1,0:T(8,128)(2,1)S(1)}, bf16[2,128,2048]{2,1,0:T(8,128)(2,1)S(1)}, u32[]{:S(2)}, u32[]{:S(2)}) collective-permute-start(bf16[2,128,2048]{2,1,0:T(8,128)(2,1)S(1)} %get-tuple-element.91.saved_ref.refs_5_.refs_6_.refs_10_), channel_id=1, source_target_pairs={{0,2},{2,0},{4,6},{6,4},{1,3},{3,1},{5,7},{7,5},{8,10},{10,8},{12,... | collective-permute-start | bytes 3145736 | tf_op jit(solution)/shard_map/ppermute | solution.py:75
  45.3 1.6 %collective-permute-start.12 = (bf16[128,1024]{1,0:T(8,128)(2,1)S(1)}, bf16[128,1024]{1,0:T(8,128)(2,1)S(1)}, u32[]{:S(2)}, u32[]{:S(2)}) collective-permute-start(bf16[128,1024]{1,0:T(8,128)(2,1)S(1)} %get-tuple-element.60), channel_id=1, source_target_pairs={{0,24},{8,0},{16,8},{24,16},{1,25},{9,1},{17,9},{25,17},{2,26},{10... | collective-permute-start | bytes 786440 | tf_op jit(solution)/shard_map/ppermute | solution.py:44
  49.4 6.6 %collective-permute-done.28.first_ref.refs_11_ = bf16[1,128,2048]{2,1,0:T(8,128)(2,1)S(1)} collective-permute-done((bf16[1,128,2048]{2,1,0:T(8,128)(2,1)S(1)}, bf16[1,128,2048]{2,1,0:T(8,128)(2,1)S(1)}, u32[]{:S(2)}, u32[]{:S(2)}) %collective-permute-start.28) | collective-permute-done | bytes 524320 | tf_op jit(solution)/shard_map/ppermute | solution.py:75
  60.7 21.4 %collective-permute-done.18.first_ref.refs_11_ = bf16[1,128,2048]{2,1,0:T(8,128)(2,1)S(1)} collective-permute-done((bf16[1,128,2048]{2,1,0:T(8,128)(2,1)S(1)}, bf16[1,128,2048]{2,1,0:T(8,128)(2,1)S(1)}, u32[]{:S(2)}, u32[]{:S(2)}) %collective-permute-start.18) | collective-permute-done | bytes 524320 | tf_op jit(solution)/shard_map/ppermute | solution.py:75
  84.9 1.6 %shard_map.130.refs_3_ = bf16[512,384]{1,0:T(8,128)(2,1)S(1)} custom-call(bf16[1,128,2048]{2,1,0:T(8,128)(2,1)S(1)} %collective-permute-done.18.first_ref.refs_11_, bf16[2,128,2048]{2,1,0:T(8,128)(2,1)S(1)} %collective-permute-done.19.later_ref.refs_12_, bf16[128,2048]{1,0:T(8,128)(2,1)S(1)} %collective-permute-done.20.cot_ref.refs_8_, ...), custom_call_target="tpu_custom_call" | custom-call | flops 536870912 | tf_op jit(solution)/shard_map/pallas_call | solution.py:23
  86.5 6.8 %collective-permute-done.22.refs_0_.refs_9_ = bf16[128,2048]{1,0:T(8,128)(2,1)S(1)} collective-permute-done((bf16[128,2048]{1,0:T(8,128)(2,1)S(1)}, bf16[128,2048]{1,0:T(8,128)(2,1)S(1)}, u32[]{:S(2)}, u32[]{:S(2)}) %collective-permute-start.22) | collective-permute-done | bytes 524320 | tf_op jit(solution)/shard_map/ppermute | solution.py:75
  93.3 1.6 %shard_map.134.refs_3_ = bf16[512,384]{1,0:T(8,128)(2,1)S(1)} custom-call(bf16[1,128,2048]{2,1,0:T(8,128)(2,1)S(1)} %collective-permute-done.28.first_ref.refs_11_, bf16[2,128,2048]{2,1,0:T(8,128)(2,1)S(1)} %collective-permute-done.29.later_ref.refs_12_, bf16[128,2048]{1,0:T(8,128)(2,1)S(1)} %collective-permute-done.30.cot_ref.refs_8_, ...), custom_call_target="tpu_custom_call" | custom-call | flops 536870912 | tf_op jit(solution)/shard_map/pallas_call | solution.py:23
  96.3 2.6 %collective-permute-done.24.refs_0_.refs_10_ = bf16[128,1024]{1,0:T(8,128)(2,1)S(1)} collective-permute-done((bf16[128,1024]{1,0:T(8,128)(2,1)S(1)}, bf16[128,1024]{1,0:T(8,128)(2,1)S(1)}, u32[]{:S(2)}, u32[]{:S(2)}) %collective-permute-start.24) | collective-permute-done | bytes 262176 | tf_op jit(solution)/shard_map/ppermute | solution.py:75
  99.4 3.9 %collective-permute-done.25.refs_1_.refs_10_ = bf16[128,1024]{1,0:T(8,128)(2,1)S(1)} collective-permute-done((bf16[128,1024]{1,0:T(8,128)(2,1)S(1)}, bf16[128,1024]{1,0:T(8,128)(2,1)S(1)}, u32[]{:S(2)}, u32[]{:S(2)}) %collective-permute-start.25) | collective-permute-done | bytes 262176 | tf_op jit(solution)/shard_map/ppermute | solution.py:75
  106.0 1.8 %shard_map.129 = (bf16[2,128,2048]{2,1,0:T(8,128)(2,1)}, bf16[2,256,128]{2,1,0:T(8,128)(2,1)S(1)}) custom-call(bf16[128,640]{1,0:T(8,128)(2,1)S(1)} %shard_map.124.refs_0_, bf16[128,640]{1,0:T(8,128)(2,1)S(1)} %collective-permute-done.11.refs_1_, bf16[128,512]{1,0:T(8,128)(2,1)S(1)} %shard_map.125.refs_2_, ...), custom_call_target="tpu_custom_call" | custom-call | flops 268435456 | tf_op jit(solution)/shard_map/pallas_call | solution.py:23
  110.3 1.6 %collective-permute-start.42 = (bf16[128,1024]{1,0:T(8,128)(2,1)S(1)}, bf16[128,1024]{1,0:T(8,128)(2,1)S(1)}, u32[]{:S(2)}, u32[]{:S(2)}) collective-permute-start(bf16[128,1024]{1,0:T(8,128)(2,1)S(1)} %get-tuple-element.83), channel_id=1, source_target_pairs={{0,4},{2,6},{4,0},{6,2},{1,5},{3,7},{5,1},{7,3},{8,12},{10,14},{12... | collective-permute-start | bytes 786440 | tf_op jit(solution)/shard_map/ppermute | solution.py:83
  113.2 1.6 %collective-permute-start.43 = (bf16[128,1024]{1,0:T(8,128)(2,1)S(1)}, bf16[128,1024]{1,0:T(8,128)(2,1)S(1)}, u32[]{:S(2)}, u32[]{:S(2)}) collective-permute-start(bf16[128,1024]{1,0:T(8,128)(2,1)S(1)} %get-tuple-element.85), channel_id=1, source_target_pairs={{0,2},{4,6},{2,0},{6,4},{1,3},{5,7},{3,1},{7,5},{8,10},{12,14},{10... | collective-permute-start | bytes 786440 | tf_op jit(solution)/shard_map/ppermute | solution.py:83
  119.3 1.6 %collective-permute-start.38 = (bf16[128,1024]{1,0:T(8,128)(2,1)S(1)}, bf16[128,1024]{1,0:T(8,128)(2,1)S(1)}, u32[]{:S(2)}, u32[]{:S(2)}) collective-permute-start(bf16[128,1024]{1,0:T(8,128)(2,1)S(1)} %get-tuple-element.75), channel_id=1, source_target_pairs={{0,4},{2,6},{4,0},{6,2},{1,5},{3,7},{5,1},{7,3},{8,12},{10,14},{12... | collective-permute-start | bytes 786440 | tf_op jit(solution)/shard_map/ppermute | solution.py:83
  122.5 1.5 %collective-permute-start.39 = (bf16[128,1024]{1,0:T(8,128)(2,1)S(1)}, bf16[128,1024]{1,0:T(8,128)(2,1)S(1)}, u32[]{:S(2)}, u32[]{:S(2)}) collective-permute-start(bf16[128,1024]{1,0:T(8,128)(2,1)S(1)} %get-tuple-element.77), channel_id=1, source_target_pairs={{0,2},{4,6},{2,0},{6,4},{1,3},{5,7},{3,1},{7,5},{8,10},{12,14},{10... | collective-permute-start | bytes 786440 | tf_op jit(solution)/shard_map/ppermute | solution.py:83
  125.1 1.6 %collective-permute-start.27 = (bf16[128,1024]{1,0:T(8,128)(2,1)S(1)}, bf16[128,1024]{1,0:T(8,128)(2,1)S(1)}, u32[]{:S(2)}, u32[]{:S(2)}) collective-permute-start(bf16[128,1024]{1,0:T(8,128)(2,1)S(1)} %get-tuple-element.68), channel_id=1, source_target_pairs={{0,4},{2,6},{4,0},{6,2},{1,5},{3,7},{5,1},{7,3},{8,12},{10,14},{12... | collective-permute-start | bytes 786440 | tf_op jit(solution)/shard_map/ppermute | solution.py:83
  131.2 4.5 %collective-permute-done.39.refs_3_ = bf16[128,1024]{1,0:T(8,128)(2,1)S(1)} collective-permute-done((bf16[128,1024]{1,0:T(8,128)(2,1)S(1)}, bf16[128,1024]{1,0:T(8,128)(2,1)S(1)}, u32[]{:S(2)}, u32[]{:S(2)}) %collective-permute-start.39) | collective-permute-done | bytes 262176 | tf_op jit(solution)/shard_map/ppermute | solution.py:83
  136.8 3.3 %collective-permute-done.37.refs_3_ = bf16[128,1024]{1,0:T(8,128)(2,1)S(1)} collective-permute-done((bf16[128,1024]{1,0:T(8,128)(2,1)S(1)}, bf16[128,1024]{1,0:T(8,128)(2,1)S(1)}, u32[]{:S(2)}, u32[]{:S(2)}) %collective-permute-start.37) | collective-permute-done | bytes 262176 | tf_op jit(solution)/shard_map/ppermute | solution.py:83
  (114 shorter events, 52.9 us)
Async XLA Ops:
  10.1 19.9 %collective-permute-start.6 = (bf16[128,2048]{1,0:T(8,128)(2,1)S(1)}, bf16[128,2048]{1,0:T(8,128)(2,1)S(1)}, u32[]{:S(2)}, u32[]{:S(2)}) collective-permute-start(bf16[128,2048]{1,0:T(8,128)(2,1)S(1)} %get-tuple-element.51.refs_8_), channel_id=1, source_target_pairs={{8,0},{16,8},{24,16},{9,1},{17,9},{25,17},{10,2},{18,10},{26,18},{... | collective-permute-start | bytes 1572872 | tf_op jit(solution)/shard_map/ppermute | solution.py:484
  12.4 26.0 %collective-permute-start.3 = (bf16[128,2048]{1,0:T(8,128)(2,1)S(1)}, bf16[128,2048]{1,0:T(8,128)(2,1)S(1)}, u32[]{:S(2)}, u32[]{:S(2)}) collective-permute-start(bf16[128,2048]{1,0:T(8,128)(2,1)S(1)} %get-tuple-element.53), channel_id=1, source_target_pairs={{0,24},{8,0},{16,8},{24,16},{1,25},{9,1},{17,9},{25,17},{2,26},{10... | collective-permute-start | bytes 1572872 | tf_op jit(solution)/shard_map/ppermute | solution.py:44
  30.0 15.3 %collective-permute-start.30 = (bf16[128,2048]{1,0:T(8,128)(2,1)S(1)}, bf16[128,2048]{1,0:T(8,128)(2,1)S(1)}, u32[]{:S(2)}, u32[]{:S(2)}) collective-permute-start(bf16[128,2048]{1,0:T(8,128)(2,1)S(1)} %get-tuple-element.92.cot_ref.refs_4_.refs_5_), channel_id=1, source_target_pairs={{0,4},{4,0},{2,6},{6,2},{1,5},{5,1},{3,7},{7,3},{8,12},{12,8},{10,... | collective-permute-start | bytes 1572872 | tf_op jit(solution)/shard_map/ppermute | solution.py:75
  33.5 14.9 %collective-permute-start.20 = (bf16[128,2048]{1,0:T(8,128)(2,1)S(1)}, bf16[128,2048]{1,0:T(8,128)(2,1)S(1)}, u32[]{:S(2)}, u32[]{:S(2)}) collective-permute-start(bf16[128,2048]{1,0:T(8,128)(2,1)S(1)} %get-tuple-element.93.cot_ref.refs_4_.refs_5_), channel_id=1, source_target_pairs={{0,2},{2,0},{4,6},{6,4},{1,3},{3,1},{5,7},{7,5},{8,10},{10,8},{12,... | collective-permute-start | bytes 1572872 | tf_op jit(solution)/shard_map/ppermute | solution.py:75
  39.8 16.2 %collective-permute-start.28 = (bf16[1,128,2048]{2,1,0:T(8,128)(2,1)S(1)}, bf16[1,128,2048]{2,1,0:T(8,128)(2,1)S(1)}, u32[]{:S(2)}, u32[]{:S(2)}) collective-permute-start(bf16[1,128,2048]{2,1,0:T(8,128)(2,1)S(1)} %get-tuple-element.49.refs_5_.refs_9_), channel_id=1, source_target_pairs={{0,4},{4,0},{2,6},{6,2},{1,5},{5,1},{3,7},{7,3},{8,12},{12,8},{10,... | collective-permute-start | bytes 1572872 | tf_op jit(solution)/shard_map/ppermute | solution.py:75
  41.5 40.6 %collective-permute-start.29 = (bf16[2,128,2048]{2,1,0:T(8,128)(2,1)S(1)}, bf16[2,128,2048]{2,1,0:T(8,128)(2,1)S(1)}, u32[]{:S(2)}, u32[]{:S(2)}) collective-permute-start(bf16[2,128,2048]{2,1,0:T(8,128)(2,1)S(1)} %get-tuple-element.90.saved_ref.refs_5_.refs_6_.refs_10_), channel_id=1, source_target_pairs={{0,4},{4,0},{2,6},{6,2},{1,5},{5,1},{3,7},{7,3},{8,12},{12,8},{10,... | collective-permute-start | bytes 3145736 | tf_op jit(solution)/shard_map/ppermute | solution.py:75
  41.8 40.8 %collective-permute-start.19 = (bf16[2,128,2048]{2,1,0:T(8,128)(2,1)S(1)}, bf16[2,128,2048]{2,1,0:T(8,128)(2,1)S(1)}, u32[]{:S(2)}, u32[]{:S(2)}) collective-permute-start(bf16[2,128,2048]{2,1,0:T(8,128)(2,1)S(1)} %get-tuple-element.91.saved_ref.refs_5_.refs_6_.refs_10_), channel_id=1, source_target_pairs={{0,2},{2,0},{4,6},{6,4},{1,3},{3,1},{5,7},{7,5},{8,10},{10,8},{12,... | collective-permute-start | bytes 3145736 | tf_op jit(solution)/shard_map/ppermute | solution.py:75
  45.3 12.2 %collective-permute-start.12 = (bf16[128,1024]{1,0:T(8,128)(2,1)S(1)}, bf16[128,1024]{1,0:T(8,128)(2,1)S(1)}, u32[]{:S(2)}, u32[]{:S(2)}) collective-permute-start(bf16[128,1024]{1,0:T(8,128)(2,1)S(1)} %get-tuple-element.60), channel_id=1, source_target_pairs={{0,24},{8,0},{16,8},{24,16},{1,25},{9,1},{17,9},{25,17},{2,26},{10... | collective-permute-start | bytes 786440 | tf_op jit(solution)/shard_map/ppermute | solution.py:44
  56.0 26.1 %collective-permute-start.18 = (bf16[1,128,2048]{2,1,0:T(8,128)(2,1)S(1)}, bf16[1,128,2048]{2,1,0:T(8,128)(2,1)S(1)}, u32[]{:S(2)}, u32[]{:S(2)}) collective-permute-start(bf16[1,128,2048]{2,1,0:T(8,128)(2,1)S(1)} %get-tuple-element.45.refs_0_.refs_5_.refs_9_), channel_id=1, source_target_pairs={{0,2},{2,0},{4,6},{6,4},{1,3},{3,1},{5,7},{7,5},{8,10},{10,8},{12,... | collective-permute-start | bytes 1572872 | tf_op jit(solution)/shard_map/ppermute | solution.py:75
  57.5 35.8 %collective-permute-start.22 = (bf16[128,2048]{1,0:T(8,128)(2,1)S(1)}, bf16[128,2048]{1,0:T(8,128)(2,1)S(1)}, u32[]{:S(2)}, u32[]{:S(2)}) collective-permute-start(bf16[128,2048]{1,0:T(8,128)(2,1)S(1)} %collective-permute-done.3.refs_0_.refs_4_.refs_6_), channel_id=1, source_target_pairs={{0,2},{2,0},{4,6},{6,4},{1,3},{3,1},{5,7},{7,5},{8,10},{10,8},{12,... | collective-permute-start | bytes 1572872 | tf_op jit(solution)/shard_map/ppermute | solution.py:75
  58.4 36.5 %collective-permute-start.16 = (bf16[128,2048]{1,0:T(8,128)(2,1)S(1)}, bf16[128,2048]{1,0:T(8,128)(2,1)S(1)}, u32[]{:S(2)}, u32[]{:S(2)}) collective-permute-start(bf16[128,2048]{1,0:T(8,128)(2,1)S(1)} %get-tuple-element.58.refs_8_), channel_id=1, source_target_pairs={{8,0},{16,8},{24,16},{9,1},{17,9},{25,17},{10,2},{18,10},{26,18},{... | collective-permute-start | bytes 1572872 | tf_op jit(solution)/shard_map/ppermute | solution.py:484
  82.1 27.6 %collective-permute-start.32 = (bf16[128,2048]{1,0:T(8,128)(2,1)S(1)}, bf16[128,2048]{1,0:T(8,128)(2,1)S(1)}, u32[]{:S(2)}, u32[]{:S(2)}) collective-permute-start(bf16[128,2048]{1,0:T(8,128)(2,1)S(1)} %get-tuple-element.57.refs_4_.refs_6_), channel_id=1, source_target_pairs={{0,4},{4,0},{2,6},{6,2},{1,5},{5,1},{3,7},{7,3},{8,12},{12,8},{10,... | collective-permute-start | bytes 1572872 | tf_op jit(solution)/shard_map/ppermute | solution.py:75
  82.6 16.3 %collective-permute-start.24 = (bf16[128,1024]{1,0:T(8,128)(2,1)S(1)}, bf16[128,1024]{1,0:T(8,128)(2,1)S(1)}, u32[]{:S(2)}, u32[]{:S(2)}) collective-permute-start(bf16[128,1024]{1,0:T(8,128)(2,1)S(1)} %collective-permute-done.12.refs_0_.refs_4_.refs_7_), channel_id=1, source_target_pairs={{0,2},{2,0},{4,6},{6,4},{1,3},{3,1},{5,7},{7,5},{8,10},{10,8},{12,... | collective-permute-start | bytes 786440 | tf_op jit(solution)/shard_map/ppermute | solution.py:75
  84.1 19.3 %collective-permute-start.25 = (bf16[128,1024]{1,0:T(8,128)(2,1)S(1)}, bf16[128,1024]{1,0:T(8,128)(2,1)S(1)}, u32[]{:S(2)}, u32[]{:S(2)}) collective-permute-start(bf16[128,1024]{1,0:T(8,128)(2,1)S(1)} %collective-permute-done.13.refs_1_.refs_5_.refs_7_), channel_id=1, source_target_pairs={{0,2},{2,0},{4,6},{6,4},{1,3},{3,1},{5,7},{7,5},{8,10},{10,8},{12,... | collective-permute-start | bytes 786440 | tf_op jit(solution)/shard_map/ppermute | solution.py:75
  93.3 14.6 %collective-permute-start.21 = (bf16[512,384]{1,0:T(8,128)(2,1)S(1)}, bf16[512,384]{1,0:T(8,128)(2,1)S(1)}, u32[]{:S(2)}, u32[]{:S(2)}) collective-permute-start(bf16[512,384]{1,0:T(8,128)(2,1)S(1)} %shard_map.130.refs_3_), channel_id=1, source_target_pairs={{0,1},{1,0},{2,3},{3,2},{4,5},{5,4},{6,7},{7,6},{8,9},{9,8},{10,11... | collective-permute-start | bytes 1179656 | tf_op jit(solution)/shard_map/ppermute | solution.py:52
  94.9 15.4 %collective-permute-start.31 = (bf16[512,384]{1,0:T(8,128)(2,1)S(1)}, bf16[512,384]{1,0:T(8,128)(2,1)S(1)}, u32[]{:S(2)}, u32[]{:S(2)}) collective-permute-start(bf16[512,384]{1,0:T(8,128)(2,1)S(1)} %shard_map.134.refs_3_), channel_id=1, source_target_pairs={{0,1},{1,0},{2,3},{3,2},{4,5},{5,4},{6,7},{7,6},{8,9},{9,8},{10,11... | collective-permute-start | bytes 1179656 | tf_op jit(solution)/shard_map/ppermute | solution.py:52
  98.9 12.9 %collective-permute-start.34 = (bf16[128,1024]{1,0:T(8,128)(2,1)S(1)}, bf16[128,1024]{1,0:T(8,128)(2,1)S(1)}, u32[]{:S(2)}, u32[]{:S(2)}) collective-permute-start(bf16[128,1024]{1,0:T(8,128)(2,1)S(1)} %get-tuple-element.63.refs_4_.refs_7_), channel_id=1, source_target_pairs={{0,4},{4,0},{2,6},{6,2},{1,5},{5,1},{3,7},{7,3},{8,12},{12,8},{10,... | collective-permute-start | bytes 786440 | tf_op jit(solution)/shard_map/ppermute | solution.py:75
  110.3 12.2 %collective-permute-start.42 = (bf16[128,1024]{1,0:T(8,128)(2,1)S(1)}, bf16[128,1024]{1,0:T(8,128)(2,1)S(1)}, u32[]{:S(2)}, u32[]{:S(2)}) collective-permute-start(bf16[128,1024]{1,0:T(8,128)(2,1)S(1)} %get-tuple-element.83), channel_id=1, source_target_pairs={{0,4},{2,6},{4,0},{6,2},{1,5},{3,7},{5,1},{7,3},{8,12},{10,14},{12... | collective-permute-start | bytes 786440 | tf_op jit(solution)/shard_map/ppermute | solution.py:83
  111.8 13.2 %collective-permute-start.40 = (bf16[128,1024]{1,0:T(8,128)(2,1)S(1)}, bf16[128,1024]{1,0:T(8,128)(2,1)S(1)}, u32[]{:S(2)}, u32[]{:S(2)}) collective-permute-start(bf16[128,1024]{1,0:T(8,128)(2,1)S(1)} %get-tuple-element.79), channel_id=1, source_target_pairs={{0,4},{2,6},{4,0},{6,2},{1,5},{3,7},{5,1},{7,3},{8,12},{10,14},{12... | collective-permute-start | bytes 786440 | tf_op jit(solution)/shard_map/ppermute | solution.py:83
  113.2 13.4 %collective-permute-start.43 = (bf16[128,1024]{1,0:T(8,128)(2,1)S(1)}, bf16[128,1024]{1,0:T(8,128)(2,1)S(1)}, u32[]{:S(2)}, u32[]{:S(2)}) collective-permute-start(bf16[128,1024]{1,0:T(8,128)(2,1)S(1)} %get-tuple-element.85), channel_id=1, source_target_pairs={{0,2},{4,6},{2,0},{6,4},{1,3},{5,7},{3,1},{7,5},{8,10},{12,14},{10... | collective-permute-start | bytes 786440 | tf_op jit(solution)/shard_map/ppermute | solution.py:83
  119.3 11.8 %collective-permute-start.38 = (bf16[128,1024]{1,0:T(8,128)(2,1)S(1)}, bf16[128,1024]{1,0:T(8,128)(2,1)S(1)}, u32[]{:S(2)}, u32[]{:S(2)}) collective-permute-start(bf16[128,1024]{1,0:T(8,128)(2,1)S(1)} %get-tuple-element.75), channel_id=1, source_target_pairs={{0,4},{2,6},{4,0},{6,2},{1,5},{3,7},{5,1},{7,3},{8,12},{10,14},{12... | collective-permute-start | bytes 786440 | tf_op jit(solution)/shard_map/ppermute | solution.py:83
  122.5 13.2 %collective-permute-start.39 = (bf16[128,1024]{1,0:T(8,128)(2,1)S(1)}, bf16[128,1024]{1,0:T(8,128)(2,1)S(1)}, u32[]{:S(2)}, u32[]{:S(2)}) collective-permute-start(bf16[128,1024]{1,0:T(8,128)(2,1)S(1)} %get-tuple-element.77), channel_id=1, source_target_pairs={{0,2},{4,6},{2,0},{6,4},{1,3},{5,7},{3,1},{7,5},{8,10},{12,14},{10... | collective-permute-start | bytes 786440 | tf_op jit(solution)/shard_map/ppermute | solution.py:83
  125.1 11.7 %collective-permute-start.27 = (bf16[128,1024]{1,0:T(8,128)(2,1)S(1)}, bf16[128,1024]{1,0:T(8,128)(2,1)S(1)}, u32[]{:S(2)}, u32[]{:S(2)}) collective-permute-start(bf16[128,1024]{1,0:T(8,128)(2,1)S(1)} %get-tuple-element.68), channel_id=1, source_target_pairs={{0,4},{2,6},{4,0},{6,2},{1,5},{3,7},{5,1},{7,3},{8,12},{10,14},{12... | collective-permute-start | bytes 786440 | tf_op jit(solution)/shard_map/ppermute | solution.py:83
  126.6 13.5 %collective-permute-start.37 = (bf16[128,1024]{1,0:T(8,128)(2,1)S(1)}, bf16[128,1024]{1,0:T(8,128)(2,1)S(1)}, u32[]{:S(2)}, u32[]{:S(2)}) collective-permute-start(bf16[128,1024]{1,0:T(8,128)(2,1)S(1)} %get-tuple-element.73), channel_id=1, source_target_pairs={{0,2},{4,6},{2,0},{6,4},{1,3},{5,7},{3,1},{7,5},{8,10},{12,14},{10... | collective-permute-start | bytes 786440 | tf_op jit(solution)/shard_map/ppermute | solution.py:83
  (26 other events, 133.4 us)

commit v2 on v1

--- a/solution.py
+++ b/solution.py
@@ -518,6 +518,7 @@
     grads = []
     for k in (0, 1):
         splits = cot_parts(steps - 1, steps)
+        shares = [width // splits] * splits if k else [width * 3 // 4, width // 4]
         parts = [[] for _ in range(splits)]
         for v in range(2):
             if k:
@@ -527,7 +528,7 @@
                 groups = [(x,) for x in (first_saved[v], later_saved[v], theirs_first[v], theirs_later[v], norm_gain)]
                 given = tuple(peer_backs[v])
             for i in range(splits):
-                share = width // splits
+                share, base = shares[i], sum(shares[:i])
                 own, *sends = call(
                     functools.partial(
                         grad_kernel,
@@ -537,7 +538,7 @@
                         peers,
                         full_width,
                         pairings[v],
-                        i * share,
+                        base,
                         len(groups),
                     ),
                     [shape((piece, share), f32)] + [shape((piece, share), bf16)] * (pairings[v].groups - 1),
@@ -551,7 +552,9 @@
                 parts[i] += [own] + [pairings[v].to_group(send, by + 1) for by, send in enumerate(sends)]
         total = None
         for i in range(splits):
-            total = final(scale, len(parts[i]) // 2, parts[i], shape((2, piece, width), f32), i, total)
+            total = final(
+                scale, len(parts[i]) // 2, parts[i], shape((2, piece, width), f32), sum(shares[:i]) // shares[i], total
+            )
         grads.append(total)
     return (grads[0][:, None], grads[1][:, None], leaving[:, None])
 

time: 141 us -> 146 us (1.035)
  waiting for transfers between devices: 57.8 us -> 62.3 us
    ppermute x12, waiting for transfers between devices: 42.9 us -> 22.7 us  [to_partner(): return lax.ppermute(x, DP, pairs)]
    ppermute x3, waiting for transfers between devices: 3.67 us -> 22.1 us  [moved_by(): return lax.ppermute(x, axis, [(i, (i + by) % count) for i in range(count)])]
    ppermute x8, waiting for transfers between devices: 8.87 us -> 14 us  [to_group(): return lax.ppermute(x, DP, pairs)]
    ppermute x2, waiting for transfers between devices: 0.01 us -> 2.81 us  [shards(): upper = lax.ppermute(now[1][0], PIPE, line)]
    ppermute x12, starting transfers between devices: 12.6 us -> 14.9 us  [to_partner(): return lax.ppermute(x, DP, pairs)]
    ppermute x8, starting transfers between devices: 10.3 us -> 8.5 us  [to_group(): return lax.ppermute(x, DP, pairs)]
    ppermute x19, waiting for transfers between devices: 2.36 us -> 0.66 us  [with_peers(): parts.append(lax.ppermute(part, axis, [(i, to(i)) for i in range(count)]))]
  transfers between devices with their start and end apart: 44 -> 44, of which waited for: 16 -> 13; matrix products, arithmetic and copies ran while one was open for 0% -> 0% of each run, Pallas kernels for 24% -> 23%
where the time goes in v2:
time: 146 us
  waiting for transfers between devices  62.3 us (43%)
  starting transfers between devices  43.1 us (30%)
  Pallas kernels  38.2 us (26%)
  local copies, waits for them, and re-layouts  1.55 us (1%)
    pallas_call x32, Pallas kernels, call(): pl.pallas_call(kernel, out_shape=outs, in_specs=specs or [VMEM] * len(ope...  33.9 us
    ppermute x12, waiting for transfers between devices, to_partner(): return lax.ppermute(x, DP, pairs)  22.7 us
    ppermute x3, waiting for transfers between devices, moved_by(): return lax.ppermute(x, axis, [(i, (i + by) % count) for i in range(count)])  22.1 us
    ppermute x12, starting transfers between devices, to_partner(): return lax.ppermute(x, DP, pairs)  14.9 us
    ppermute x8, waiting for transfers between devices, to_group(): return lax.ppermute(x, DP, pairs)  14 us
    ppermute x3, starting transfers between devices, moved_by(): return lax.ppermute(x, axis, [(i, (i + by) % count) for i in range(count)])  8.73 us
    ppermute x8, starting transfers between devices, to_group(): return lax.ppermute(x, DP, pairs)  8.5 us
    ppermute x19, starting transfers between devices, with_peers(): parts.append(lax.ppermute(part, axis, [(i, to(i)) for i in range(count)]))  8.22 us
  transfers between devices with their start and end apart: 44, of which 13 were waited for; matrix products, arithmetic and copies ran while one was open for 0% of the time, Pallas kernels for 23%

profile of v2, /device:TPU:0, one launch (start us, length us, event | category | flops | bytes accessed | tf_op | source)
XLA Modules:
  0.0 146.2 jit_solution(17150170605377469967)
XLA Ops:
  1.9 3.6 %shard_map.112 = (bf16[256,640]{1,0:T(8,128)(2,1)S(1)}, bf16[512,2048]{1,0:T(8,128)(2,1)S(1)}, bf16[512,2048]{1,0:T(8,128)(2,1)S(1)}, bf16[1,128,2048]{2,1,0:T(8,128)(2,1)S(1)}, bf16[1,128,2048]{2,1,0:T(8,128)(2,1)S(1)}) custom-call(bf16[3,2,1,128,2048]{4,3,2,1,0:T(8,128)(2,1)} %saved_ref.3, bf16[2,1,512,2048]{3,2,1,0:T(8,128)(2,1)} %proj_in_ref.3, ...), custom_call_target="tpu_custom_call" | custom-call | flops 536870912 | tf_op jit(solution)/shard_map/pallas_call | solution.py:23
  7.9 4.0 %collective-permute-start.9 = (f32[8,128]{1,0:T(8,128)S(1)}, f32[8,128]{1,0:T(8,128)S(1)}, u32[]{:S(2)}, u32[]{:S(2)}) collective-permute-start(f32[8,128]{1,0:T(8,128)S(1)} %shard_map.119.refs_0_), channel_id=1, source_target_pairs={{0,6},{2,4},{4,2},{6,0},{1,7},{3,5},{5,3},{7,1},{8,14},{10,12},{12... | collective-permute-start | bytes 12296 | tf_op jit(solution)/shard_map/ppermute | solution.py:52
  13.4 3.3 %shard_map.113 = (bf16[256,640]{1,0:T(8,128)(2,1)S(1)}, bf16[512,2048]{1,0:T(8,128)(2,1)S(1)}, bf16[512,2048]{1,0:T(8,128)(2,1)S(1)}) custom-call(bf16[3,2,1,128,2048]{4,3,2,1,0:T(8,128)(2,1)} %saved_ref.3, bf16[2,1,512,2048]{3,2,1,0:T(8,128)(2,1)} %proj_in_ref.3, bf16[2,1,512,2048]{3,2,1,0:T(8,128)(2,1)} %proj_out_ref.3, f32[2,1,2048]{2,1,0:T(1,128)S(1)} %copy-done, ...), custom_call_target="tpu_custom_call" | custom-call | flops 536870912 | tf_op jit(solution)/shard_map/pallas_call | solution.py:23
  17.3 2.0 %collective-permute-start.30 = (bf16[128,2048]{1,0:T(8,128)(2,1)S(1)}, bf16[128,2048]{1,0:T(8,128)(2,1)S(1)}, u32[]{:S(2)}, u32[]{:S(2)}) collective-permute-start(bf16[128,2048]{1,0:T(8,128)(2,1)S(1)} %get-tuple-element.92.cot_ref.refs_4_.refs_5_), channel_id=1, source_target_pairs={{0,4},{4,0},{2,6},{6,2},{1,5},{5,1},{3,7},{7,3},{8,12},{12,8},{10,... | collective-permute-start | bytes 1572872 | tf_op jit(solution)/shard_map/ppermute | solution.py:75
  26.9 5.2 %collective-permute-done.30.cot_ref.refs_8_ = bf16[128,2048]{1,0:T(8,128)(2,1)S(1)} collective-permute-done((bf16[128,2048]{1,0:T(8,128)(2,1)S(1)}, bf16[128,2048]{1,0:T(8,128)(2,1)S(1)}, u32[]{:S(2)}, u32[]{:S(2)}) %collective-permute-start.30) | collective-permute-done | bytes 524320 | tf_op jit(solution)/shard_map/ppermute | solution.py:75
  32.1 4.1 %collective-permute-start.3 = (bf16[128,2048]{1,0:T(8,128)(2,1)S(1)}, bf16[128,2048]{1,0:T(8,128)(2,1)S(1)}, u32[]{:S(2)}, u32[]{:S(2)}) collective-permute-start(bf16[128,2048]{1,0:T(8,128)(2,1)S(1)} %get-tuple-element.53), channel_id=1, source_target_pairs={{0,24},{8,0},{16,8},{24,16},{1,25},{9,1},{17,9},{25,17},{2,26},{10... | collective-permute-start | bytes 1572872 | tf_op jit(solution)/shard_map/ppermute | solution.py:44
  37.7 2.8 %collective-permute-done.6.got_ref = bf16[128,2048]{1,0:T(8,128)(2,1)S(1)} collective-permute-done((bf16[128,2048]{1,0:T(8,128)(2,1)S(1)}, bf16[128,2048]{1,0:T(8,128)(2,1)S(1)}, u32[]{:S(2)}, u32[]{:S(2)}) %collective-permute-start.6) | collective-permute-done | bytes 524320 | tf_op jit(solution)/shard_map/ppermute | solution.py:484
  43.1 8.1 %collective-permute-done.3.refs_0_.refs_4_.refs_6_ = bf16[128,2048]{1,0:T(8,128)(2,1)S(1)} collective-permute-done((bf16[128,2048]{1,0:T(8,128)(2,1)S(1)}, bf16[128,2048]{1,0:T(8,128)(2,1)S(1)}, u32[]{:S(2)}, u32[]{:S(2)}) %collective-permute-start.3) | collective-permute-done | bytes 524320 | tf_op jit(solution)/shard_map/ppermute | solution.py:44
  53.4 11.7 %collective-permute-done.28.first_ref.refs_11_ = bf16[1,128,2048]{2,1,0:T(8,128)(2,1)S(1)} collective-permute-done((bf16[1,128,2048]{2,1,0:T(8,128)(2,1)S(1)}, bf16[1,128,2048]{2,1,0:T(8,128)(2,1)S(1)}, u32[]{:S(2)}, u32[]{:S(2)}) %collective-permute-start.28) | collective-permute-done | bytes 524320 | tf_op jit(solution)/shard_map/ppermute | solution.py:75
  66.5 1.8 %collective-permute-done.18.first_ref.refs_11_ = bf16[1,128,2048]{2,1,0:T(8,128)(2,1)S(1)} collective-permute-done((bf16[1,128,2048]{2,1,0:T(8,128)(2,1)S(1)}, bf16[1,128,2048]{2,1,0:T(8,128)(2,1)S(1)}, u32[]{:S(2)}, u32[]{:S(2)}) %collective-permute-start.18) | collective-permute-done | bytes 524320 | tf_op jit(solution)/shard_map/ppermute | solution.py:75
  68.5 1.7 %collective-permute-start.22 = (bf16[128,2048]{1,0:T(8,128)(2,1)S(1)}, bf16[128,2048]{1,0:T(8,128)(2,1)S(1)}, u32[]{:S(2)}, u32[]{:S(2)}) collective-permute-start(bf16[128,2048]{1,0:T(8,128)(2,1)S(1)} %collective-permute-done.3.refs_0_.refs_4_.refs_6_), channel_id=1, source_target_pairs={{0,2},{2,0},{4,6},{6,4},{1,3},{3,1},{5,7},{7,5},{8,10},{10,8},{12,... | collective-permute-start | bytes 1572872 | tf_op jit(solution)/shard_map/ppermute | solution.py:75
  71.2 4.2 %collective-permute-start.12 = (bf16[128,1024]{1,0:T(8,128)(2,1)S(1)}, bf16[128,1024]{1,0:T(8,128)(2,1)S(1)}, u32[]{:S(2)}, u32[]{:S(2)}) collective-permute-start(bf16[128,1024]{1,0:T(8,128)(2,1)S(1)} %get-tuple-element.60), channel_id=1, source_target_pairs={{0,24},{8,0},{16,8},{24,16},{1,25},{9,1},{17,9},{25,17},{2,26},{10... | collective-permute-start | bytes 786440 | tf_op jit(solution)/shard_map/ppermute | solution.py:44
  75.9 11.6 %collective-permute-done.12.refs_0_.refs_4_.refs_7_ = bf16[128,1024]{1,0:T(8,128)(2,1)S(1)} collective-permute-done((bf16[128,1024]{1,0:T(8,128)(2,1)S(1)}, bf16[128,1024]{1,0:T(8,128)(2,1)S(1)}, u32[]{:S(2)}, u32[]{:S(2)}) %collective-permute-start.12) | collective-permute-done | bytes 262176 | tf_op jit(solution)/shard_map/ppermute | solution.py:44
  87.5 1.7 %collective-permute-start.24 = (bf16[128,1024]{1,0:T(8,128)(2,1)S(1)}, bf16[128,1024]{1,0:T(8,128)(2,1)S(1)}, u32[]{:S(2)}, u32[]{:S(2)}) collective-permute-start(bf16[128,1024]{1,0:T(8,128)(2,1)S(1)} %collective-permute-done.12.refs_0_.refs_4_.refs_7_), channel_id=1, source_target_pairs={{0,2},{2,0},{4,6},{6,4},{1,3},{3,1},{5,7},{7,5},{8,10},{10,8},{12,... | collective-permute-start | bytes 786440 | tf_op jit(solution)/shard_map/ppermute | solution.py:75
  89.2 2.4 %collective-permute-done.13.refs_1_.refs_5_.refs_7_ = bf16[128,1024]{1,0:T(8,128)(2,1)S(1)} collective-permute-done((bf16[128,1024]{1,0:T(8,128)(2,1)S(1)}, bf16[128,1024]{1,0:T(8,128)(2,1)S(1)}, u32[]{:S(2)}, u32[]{:S(2)}) %collective-permute-start.13) | collective-permute-done | bytes 262176 | tf_op jit(solution)/shard_map/ppermute | solution.py:44
  93.1 1.6 %shard_map.130.refs_3_ = bf16[512,384]{1,0:T(8,128)(2,1)S(1)} custom-call(bf16[1,128,2048]{2,1,0:T(8,128)(2,1)S(1)} %collective-permute-done.18.first_ref.refs_11_, bf16[2,128,2048]{2,1,0:T(8,128)(2,1)S(1)} %collective-permute-done.19.later_ref.refs_12_, bf16[128,2048]{1,0:T(8,128)(2,1)S(1)} %collective-permute-done.20.cot_ref.refs_8_, ...), custom_call_target="tpu_custom_call" | custom-call | flops 536870912 | tf_op jit(solution)/shard_map/pallas_call | solution.py:23
  96.2 1.6 %shard_map.134.refs_3_ = bf16[512,384]{1,0:T(8,128)(2,1)S(1)} custom-call(bf16[1,128,2048]{2,1,0:T(8,128)(2,1)S(1)} %collective-permute-done.28.first_ref.refs_11_, bf16[2,128,2048]{2,1,0:T(8,128)(2,1)S(1)} %collective-permute-done.29.later_ref.refs_12_, bf16[128,2048]{1,0:T(8,128)(2,1)S(1)} %collective-permute-done.30.cot_ref.refs_8_, ...), custom_call_target="tpu_custom_call" | custom-call | flops 536870912 | tf_op jit(solution)/shard_map/pallas_call | solution.py:23
  97.8 1.6 %collective-permute-start.34 = (bf16[128,1024]{1,0:T(8,128)(2,1)S(1)}, bf16[128,1024]{1,0:T(8,128)(2,1)S(1)}, u32[]{:S(2)}, u32[]{:S(2)}) collective-permute-start(bf16[128,1024]{1,0:T(8,128)(2,1)S(1)} %get-tuple-element.63.refs_4_.refs_7_), channel_id=1, source_target_pairs={{0,4},{4,0},{2,6},{6,2},{1,5},{5,1},{3,7},{7,3},{8,12},{12,8},{10,... | collective-permute-start | bytes 786440 | tf_op jit(solution)/shard_map/ppermute | solution.py:75
  99.5 1.7 %collective-permute-start.35 = (bf16[128,1024]{1,0:T(8,128)(2,1)S(1)}, bf16[128,1024]{1,0:T(8,128)(2,1)S(1)}, u32[]{:S(2)}, u32[]{:S(2)}) collective-permute-start(bf16[128,1024]{1,0:T(8,128)(2,1)S(1)} %get-tuple-element.64.refs_5_.refs_7_), channel_id=1, source_target_pairs={{0,4},{4,0},{2,6},{6,2},{1,5},{5,1},{3,7},{7,3},{8,12},{12,8},{10,... | collective-permute-start | bytes 786440 | tf_op jit(solution)/shard_map/ppermute | solution.py:75
  104.9 1.8 %shard_map.129 = (bf16[2,128,2048]{2,1,0:T(8,128)(2,1)}, bf16[2,256,128]{2,1,0:T(8,128)(2,1)S(1)}) custom-call(bf16[128,640]{1,0:T(8,128)(2,1)S(1)} %shard_map.124.refs_0_, bf16[128,640]{1,0:T(8,128)(2,1)S(1)} %collective-permute-done.11.refs_1_, bf16[128,512]{1,0:T(8,128)(2,1)S(1)} %shard_map.125.refs_2_, ...), custom_call_target="tpu_custom_call" | custom-call | flops 268435456 | tf_op jit(solution)/shard_map/pallas_call | solution.py:23
  108.2 3.9 %collective-permute-done.35.refs_1_.refs_10_ = bf16[128,1024]{1,0:T(8,128)(2,1)S(1)} collective-permute-done((bf16[128,1024]{1,0:T(8,128)(2,1)S(1)}, bf16[128,1024]{1,0:T(8,128)(2,1)S(1)}, u32[]{:S(2)}, u32[]{:S(2)}) %collective-permute-start.35) | collective-permute-done | bytes 262176 | tf_op jit(solution)/shard_map/ppermute | solution.py:75
  116.9 1.6 %collective-permute-start.38 = (bf16[128,1536]{1,0:T(8,128)(2,1)S(1)}, bf16[128,1536]{1,0:T(8,128)(2,1)S(1)}, u32[]{:S(2)}, u32[]{:S(2)}) collective-permute-start(bf16[128,1536]{1,0:T(8,128)(2,1)S(1)} %get-tuple-element.75), channel_id=1, source_target_pairs={{0,4},{2,6},{4,0},{6,2},{1,5},{3,7},{5,1},{7,3},{8,12},{10,14},{12... | collective-permute-start | bytes 1179656 | tf_op jit(solution)/shard_map/ppermute | solution.py:83
  128.5 8.9 %collective-permute-done.43.refs_3_ = bf16[128,1024]{1,0:T(8,128)(2,1)S(1)} collective-permute-done((bf16[128,1024]{1,0:T(8,128)(2,1)S(1)}, bf16[128,1024]{1,0:T(8,128)(2,1)S(1)}, u32[]{:S(2)}, u32[]{:S(2)}) %collective-permute-start.43) | collective-permute-done | bytes 262176 | tf_op jit(solution)/shard_map/ppermute | solution.py:83
  139.0 4.0 %collective-permute-done.41.refs_3_ = bf16[128,1024]{1,0:T(8,128)(2,1)S(1)} collective-permute-done((bf16[128,1024]{1,0:T(8,128)(2,1)S(1)}, bf16[128,1024]{1,0:T(8,128)(2,1)S(1)}, u32[]{:S(2)}, u32[]{:S(2)}) %collective-permute-start.41) | collective-permute-done | bytes 262176 | tf_op jit(solution)/shard_map/ppermute | solution.py:83
  (114 shorter events, 50.3 us)
Async XLA Ops:
  5.5 17.1 %collective-permute-start.1 = (bf16[256,640]{1,0:T(8,128)(2,1)S(1)}, bf16[256,640]{1,0:T(8,128)(2,1)S(1)}, u32[]{:S(2)}, u32[]{:S(2)}) collective-permute-start(bf16[256,640]{1,0:T(8,128)(2,1)S(1)} %get-tuple-element.48.refs_0_.refs_2_), channel_id=1, source_target_pairs={{0,1},{1,0},{2,3},{3,2},{4,5},{5,4},{6,7},{7,6},{8,9},{9,8},{10,11... | collective-permute-start | bytes 983048 | tf_op jit(solution)/shard_map/ppermute | solution.py:52
  7.2 13.0 %collective-permute-start.5 = (bf16[128,640]{1,0:T(8,128)(2,1)S(1)}, bf16[128,640]{1,0:T(8,128)(2,1)S(1)}, u32[]{:S(2)}, u32[]{:S(2)}) collective-permute-start(bf16[128,640]{1,0:T(8,128)(2,1)S(1)} %shard_map.118.refs_0_), channel_id=1, source_target_pairs={{0,1},{1,0},{2,3},{3,2},{4,5},{5,4},{6,7},{7,6},{8,9},{9,8},{10,11... | collective-permute-start | bytes 491528 | tf_op jit(solution)/shard_map/ppermute | solution.py:52
  17.3 14.8 %collective-permute-start.30 = (bf16[128,2048]{1,0:T(8,128)(2,1)S(1)}, bf16[128,2048]{1,0:T(8,128)(2,1)S(1)}, u32[]{:S(2)}, u32[]{:S(2)}) collective-permute-start(bf16[128,2048]{1,0:T(8,128)(2,1)S(1)} %get-tuple-element.92.cot_ref.refs_4_.refs_5_), channel_id=1, source_target_pairs={{0,4},{4,0},{2,6},{6,2},{1,5},{5,1},{3,7},{7,3},{8,12},{12,8},{10,... | collective-permute-start | bytes 1572872 | tf_op jit(solution)/shard_map/ppermute | solution.py:75
  20.2 15.9 %collective-permute-start.20 = (bf16[128,2048]{1,0:T(8,128)(2,1)S(1)}, bf16[128,2048]{1,0:T(8,128)(2,1)S(1)}, u32[]{:S(2)}, u32[]{:S(2)}) collective-permute-start(bf16[128,2048]{1,0:T(8,128)(2,1)S(1)} %get-tuple-element.93.cot_ref.refs_4_.refs_5_), channel_id=1, source_target_pairs={{0,2},{2,0},{4,6},{6,4},{1,3},{3,1},{5,7},{7,5},{8,10},{10,8},{12,... | collective-permute-start | bytes 1572872 | tf_op jit(solution)/shard_map/ppermute | solution.py:75
  23.7 16.8 %collective-permute-start.6 = (bf16[128,2048]{1,0:T(8,128)(2,1)S(1)}, bf16[128,2048]{1,0:T(8,128)(2,1)S(1)}, u32[]{:S(2)}, u32[]{:S(2)}) collective-permute-start(bf16[128,2048]{1,0:T(8,128)(2,1)S(1)} %get-tuple-element.51.refs_8_), channel_id=1, source_target_pairs={{8,0},{16,8},{24,16},{9,1},{17,9},{25,17},{10,2},{18,10},{26,18},{... | collective-permute-start | bytes 1572872 | tf_op jit(solution)/shard_map/ppermute | solution.py:484
  25.1 46.1 %collective-permute-start.29 = (bf16[2,128,2048]{2,1,0:T(8,128)(2,1)S(1)}, bf16[2,128,2048]{2,1,0:T(8,128)(2,1)S(1)}, u32[]{:S(2)}, u32[]{:S(2)}) collective-permute-start(bf16[2,128,2048]{2,1,0:T(8,128)(2,1)S(1)} %get-tuple-element.90.saved_ref.refs_5_.refs_6_.refs_10_), channel_id=1, source_target_pairs={{0,4},{4,0},{2,6},{6,2},{1,5},{5,1},{3,7},{7,3},{8,12},{12,8},{10,... | collective-permute-start | bytes 3145736 | tf_op jit(solution)/shard_map/ppermute | solution.py:75
  25.7 49.8 %collective-permute-start.19 = (bf16[2,128,2048]{2,1,0:T(8,128)(2,1)S(1)}, bf16[2,128,2048]{2,1,0:T(8,128)(2,1)S(1)}, u32[]{:S(2)}, u32[]{:S(2)}) collective-permute-start(bf16[2,128,2048]{2,1,0:T(8,128)(2,1)S(1)} %get-tuple-element.91.saved_ref.refs_5_.refs_6_.refs_10_), channel_id=1, source_target_pairs={{0,2},{2,0},{4,6},{6,4},{1,3},{3,1},{5,7},{7,5},{8,10},{10,8},{12,... | collective-permute-start | bytes 3145736 | tf_op jit(solution)/shard_map/ppermute | solution.py:75
  32.1 19.0 %collective-permute-start.3 = (bf16[128,2048]{1,0:T(8,128)(2,1)S(1)}, bf16[128,2048]{1,0:T(8,128)(2,1)S(1)}, u32[]{:S(2)}, u32[]{:S(2)}) collective-permute-start(bf16[128,2048]{1,0:T(8,128)(2,1)S(1)} %get-tuple-element.53), channel_id=1, source_target_pairs={{0,24},{8,0},{16,8},{24,16},{1,25},{9,1},{17,9},{25,17},{2,26},{10... | collective-permute-start | bytes 1572872 | tf_op jit(solution)/shard_map/ppermute | solution.py:44
  36.2 29.0 %collective-permute-start.28 = (bf16[1,128,2048]{2,1,0:T(8,128)(2,1)S(1)}, bf16[1,128,2048]{2,1,0:T(8,128)(2,1)S(1)}, u32[]{:S(2)}, u32[]{:S(2)}) collective-permute-start(bf16[1,128,2048]{2,1,0:T(8,128)(2,1)S(1)} %get-tuple-element.49.refs_5_.refs_9_), channel_id=1, source_target_pairs={{0,4},{4,0},{2,6},{6,2},{1,5},{5,1},{3,7},{7,3},{8,12},{12,8},{10,... | collective-permute-start | bytes 1572872 | tf_op jit(solution)/shard_map/ppermute | solution.py:75
  40.5 27.8 %collective-permute-start.18 = (bf16[1,128,2048]{2,1,0:T(8,128)(2,1)S(1)}, bf16[1,128,2048]{2,1,0:T(8,128)(2,1)S(1)}, u32[]{:S(2)}, u32[]{:S(2)}) collective-permute-start(bf16[1,128,2048]{2,1,0:T(8,128)(2,1)S(1)} %get-tuple-element.45.refs_0_.refs_5_.refs_9_), channel_id=1, source_target_pairs={{0,2},{2,0},{4,6},{6,4},{1,3},{3,1},{5,7},{7,5},{8,10},{10,8},{12,... | collective-permute-start | bytes 1572872 | tf_op jit(solution)/shard_map/ppermute | solution.py:75
  52.5 16.0 %collective-permute-start.4 = (bf16[128,512]{1,0:T(8,128)(2,1)S(1)}, bf16[128,512]{1,0:T(8,128)(2,1)S(1)}, u32[]{:S(2)}, u32[]{:S(2)}) collective-permute-start(bf16[128,512]{1,0:T(8,128)(2,1)S(1)} %shard_map.117.refs_2_), channel_id=1, source_target_pairs={{0,1},{1,0},{2,3},{3,2},{4,5},{5,4},{6,7},{7,6},{8,9},{9,8},{10,11... | collective-permute-start | bytes 393224 | tf_op jit(solution)/shard_map/ppermute | solution.py:52
  65.2 29.5 %collective-permute-start.16 = (bf16[128,2048]{1,0:T(8,128)(2,1)S(1)}, bf16[128,2048]{1,0:T(8,128)(2,1)S(1)}, u32[]{:S(2)}, u32[]{:S(2)}) collective-permute-start(bf16[128,2048]{1,0:T(8,128)(2,1)S(1)} %get-tuple-element.58.refs_8_), channel_id=1, source_target_pairs={{8,0},{16,8},{24,16},{9,1},{17,9},{25,17},{10,2},{18,10},{26,18},{... | collective-permute-start | bytes 1572872 | tf_op jit(solution)/shard_map/ppermute | solution.py:484
  68.3 27.3 %collective-permute-start.32 = (bf16[128,2048]{1,0:T(8,128)(2,1)S(1)}, bf16[128,2048]{1,0:T(8,128)(2,1)S(1)}, u32[]{:S(2)}, u32[]{:S(2)}) collective-permute-start(bf16[128,2048]{1,0:T(8,128)(2,1)S(1)} %get-tuple-element.57.refs_4_.refs_6_), channel_id=1, source_target_pairs={{0,4},{4,0},{2,6},{6,2},{1,5},{5,1},{3,7},{7,3},{8,12},{12,8},{10,... | collective-permute-start | bytes 1572872 | tf_op jit(solution)/shard_map/ppermute | solution.py:75
  68.5 29.2 %collective-permute-start.22 = (bf16[128,2048]{1,0:T(8,128)(2,1)S(1)}, bf16[128,2048]{1,0:T(8,128)(2,1)S(1)}, u32[]{:S(2)}, u32[]{:S(2)}) collective-permute-start(bf16[128,2048]{1,0:T(8,128)(2,1)S(1)} %collective-permute-done.3.refs_0_.refs_4_.refs_6_), channel_id=1, source_target_pairs={{0,2},{2,0},{4,6},{6,4},{1,3},{3,1},{5,7},{7,5},{8,10},{10,8},{12,... | collective-permute-start | bytes 1572872 | tf_op jit(solution)/shard_map/ppermute | solution.py:75
  71.2 16.2 %collective-permute-start.12 = (bf16[128,1024]{1,0:T(8,128)(2,1)S(1)}, bf16[128,1024]{1,0:T(8,128)(2,1)S(1)}, u32[]{:S(2)}, u32[]{:S(2)}) collective-permute-start(bf16[128,1024]{1,0:T(8,128)(2,1)S(1)} %get-tuple-element.60), channel_id=1, source_target_pairs={{0,24},{8,0},{16,8},{24,16},{1,25},{9,1},{17,9},{25,17},{2,26},{10... | collective-permute-start | bytes 786440 | tf_op jit(solution)/shard_map/ppermute | solution.py:44
  75.5 16.1 %collective-permute-start.13 = (bf16[128,1024]{1,0:T(8,128)(2,1)S(1)}, bf16[128,1024]{1,0:T(8,128)(2,1)S(1)}, u32[]{:S(2)}, u32[]{:S(2)}) collective-permute-start(bf16[128,1024]{1,0:T(8,128)(2,1)S(1)} %get-tuple-element.61), channel_id=1, source_target_pairs={{0,24},{8,0},{16,8},{24,16},{1,25},{9,1},{17,9},{25,17},{2,26},{10... | collective-permute-start | bytes 786440 | tf_op jit(solution)/shard_map/ppermute | solution.py:44
  94.6 12.1 %collective-permute-start.21 = (bf16[512,384]{1,0:T(8,128)(2,1)S(1)}, bf16[512,384]{1,0:T(8,128)(2,1)S(1)}, u32[]{:S(2)}, u32[]{:S(2)}) collective-permute-start(bf16[512,384]{1,0:T(8,128)(2,1)S(1)} %shard_map.130.refs_3_), channel_id=1, source_target_pairs={{0,1},{1,0},{2,3},{3,2},{4,5},{5,4},{6,7},{7,6},{8,9},{9,8},{10,11... | collective-permute-start | bytes 1179656 | tf_op jit(solution)/shard_map/ppermute | solution.py:52
  97.7 19.2 %collective-permute-start.31 = (bf16[512,384]{1,0:T(8,128)(2,1)S(1)}, bf16[512,384]{1,0:T(8,128)(2,1)S(1)}, u32[]{:S(2)}, u32[]{:S(2)}) collective-permute-start(bf16[512,384]{1,0:T(8,128)(2,1)S(1)} %shard_map.134.refs_3_), channel_id=1, source_target_pairs={{0,1},{1,0},{2,3},{3,2},{4,5},{5,4},{6,7},{7,6},{8,9},{9,8},{10,11... | collective-permute-start | bytes 1179656 | tf_op jit(solution)/shard_map/ppermute | solution.py:52
  99.5 12.7 %collective-permute-start.35 = (bf16[128,1024]{1,0:T(8,128)(2,1)S(1)}, bf16[128,1024]{1,0:T(8,128)(2,1)S(1)}, u32[]{:S(2)}, u32[]{:S(2)}) collective-permute-start(bf16[128,1024]{1,0:T(8,128)(2,1)S(1)} %get-tuple-element.64.refs_5_.refs_7_), channel_id=1, source_target_pairs={{0,4},{4,0},{2,6},{6,2},{1,5},{5,1},{3,7},{7,3},{8,12},{12,8},{10,... | collective-permute-start | bytes 786440 | tf_op jit(solution)/shard_map/ppermute | solution.py:75
  116.9 27.1 %collective-permute-start.38 = (bf16[128,1536]{1,0:T(8,128)(2,1)S(1)}, bf16[128,1536]{1,0:T(8,128)(2,1)S(1)}, u32[]{:S(2)}, u32[]{:S(2)}) collective-permute-start(bf16[128,1536]{1,0:T(8,128)(2,1)S(1)} %get-tuple-element.75), channel_id=1, source_target_pairs={{0,4},{2,6},{4,0},{6,2},{1,5},{3,7},{5,1},{7,3},{8,12},{10,14},{12... | collective-permute-start | bytes 1179656 | tf_op jit(solution)/shard_map/ppermute | solution.py:83
  119.7 24.4 %collective-permute-start.39 = (bf16[128,1536]{1,0:T(8,128)(2,1)S(1)}, bf16[128,1536]{1,0:T(8,128)(2,1)S(1)}, u32[]{:S(2)}, u32[]{:S(2)}) collective-permute-start(bf16[128,1536]{1,0:T(8,128)(2,1)S(1)} %get-tuple-element.77), channel_id=1, source_target_pairs={{0,2},{4,6},{2,0},{6,4},{1,3},{5,7},{3,1},{7,5},{8,10},{12,14},{10... | collective-permute-start | bytes 1179656 | tf_op jit(solution)/shard_map/ppermute | solution.py:83
  121.2 16.2 %collective-permute-start.43 = (bf16[128,1024]{1,0:T(8,128)(2,1)S(1)}, bf16[128,1024]{1,0:T(8,128)(2,1)S(1)}, u32[]{:S(2)}, u32[]{:S(2)}) collective-permute-start(bf16[128,1024]{1,0:T(8,128)(2,1)S(1)} %get-tuple-element.85), channel_id=1, source_target_pairs={{0,2},{4,6},{2,0},{6,4},{1,3},{5,7},{3,1},{7,5},{8,10},{12,14},{10... | collective-permute-start | bytes 786440 | tf_op jit(solution)/shard_map/ppermute | solution.py:83
  123.7 19.3 %collective-permute-start.41 = (bf16[128,1024]{1,0:T(8,128)(2,1)S(1)}, bf16[128,1024]{1,0:T(8,128)(2,1)S(1)}, u32[]{:S(2)}, u32[]{:S(2)}) collective-permute-start(bf16[128,1024]{1,0:T(8,128)(2,1)S(1)} %get-tuple-element.81), channel_id=1, source_target_pairs={{0,2},{4,6},{2,0},{6,4},{1,3},{5,7},{3,1},{7,5},{8,10},{12,14},{10... | collective-permute-start | bytes 786440 | tf_op jit(solution)/shard_map/ppermute | solution.py:83
  126.9 18.4 %collective-permute-start.27 = (bf16[128,512]{1,0:T(8,128)(2,1)S(1)}, bf16[128,512]{1,0:T(8,128)(2,1)S(1)}, u32[]{:S(2)}, u32[]{:S(2)}) collective-permute-start(bf16[128,512]{1,0:T(8,128)(2,1)S(1)} %get-tuple-element.68), channel_id=1, source_target_pairs={{0,4},{2,6},{4,0},{6,2},{1,5},{3,7},{5,1},{7,3},{8,12},{10,14},{12... | collective-permute-start | bytes 393224 | tf_op jit(solution)/shard_map/ppermute | solution.py:83
  (26 other events, 182.1 us)
